TPU v7x, 512 devices: a whole 4x4x16 slice. The times are simulated.
512 devices in a mesh: ia: 8 (over y, core), ja: 8 (over x, z_hi), ka: 8 (over z_lo).
Axes of the slice: x: 4, y: 4, z: 16 (z_hi: 2, z_lo: 8; z = z_hi * 8 + z_lo), core: 2. Of those that a mesh axis runs over, the one named last changes fastest.
Arguments:
- block_coords: int32 [8, 8, 8, 4, 3], P('ia', 'ja', 'ka'), may hold values from 0 to 3, as said below
- live_blocks: int32 [8, 8, 8], P('ia', 'ja', 'ka'), may hold values from 1 to 4, as said below
- counts: int32 [8, 8, 8, 4, 64, 4096], P('ia', 'ja', 'ka'), may hold values from 0 to 7
- factor_a: float32 [2048, 256], P(('ia', 'ja', 'ka')), may hold values from 0.3 to 9.6
- factor_b: float32 [2048, 256], P(('ja', 'ka')), may hold values from 0.05 to 8
- factor_c: float32 [2048, 256], P('ka', 'ia'), may hold values from 0.05 to 8
Outputs:
- factor_new: float32 [2048, 256], P(('ia', 'ja', 'ka'))
Inputs may be any that keep to these rules, and one draw needn't show every extreme that they name: `block_coords`: a device's slots name distinct blocks; slot 0 is always live, and every mode-1 block of the slab has a live block on some device. `live_blocks`: on some device all 4 slots are live.
All inputs are finite; a program needn't handle non-finite values.
Results may differ from a plain program's by a relative error of at most 0.00061.
Values may be sent and summed in bfloat16 or wider, within the bound.
No kernel may reach another device: no remote copies, remote signals or barrier semaphores. Data moves between devices by JAX's collectives and lax.ppermute only.
A program may use at most 64 MiB of HBM per device.

v0:
```python
import jax
import jax.numpy as jnp
from jax import lax
from jax.sharding import PartitionSpec as P

R = 256
BS = 64
RB1 = 4
RB2 = 4
RB3 = 4
SLOTS = 4


def from_everyone(x, axis):
    copies = jnp.broadcast_to(x, (lax.axis_size(axis), *x.shape))
    return lax.all_to_all(copies, axis, split_axis=0, concat_axis=0, tiled=True)


def laid_out(blocks, dim):
    shape = list(blocks.shape[1:])
    shape[dim] *= blocks.shape[0]
    return jnp.moveaxis(blocks, 0, dim).reshape(shape)


def collect(x, axis, dim):
    blocks = from_everyone(x, axis)
    return laid_out(blocks, dim)


def over_copies(x, axis):
    everything = from_everyone(x, axis)
    return jnp.sum(everything, axis=0)


def cut_along(x, dim, count):
    before, after = (x.shape[:dim], x.shape[dim + 1 :])
    return jnp.moveaxis(x.reshape(*before, count, -1, *after), dim, 0)


def sent_and_summed(x, axis, dim):
    blocks = cut_along(x, dim, lax.axis_size(axis))
    arrived = lax.all_to_all(blocks, axis, split_axis=0, concat_axis=0, tiled=True)
    return arrived.sum(axis=0)


def make_panel(rows_b, rows_c, index_j, index_k):
    piece_b = lax.dynamic_slice_in_dim(rows_b, index_j * BS, BS, 0)
    piece_c = lax.dynamic_slice_in_dim(rows_c, index_k * BS, BS, 0)
    return (piece_b[:, None, :] * piece_c[None, :, :]).reshape(BS * BS, R).astype(jnp.bfloat16)


def add_block(phi, factor_low, panel, index_i, weight, block_counts):
    block_a = lax.dynamic_slice_in_dim(factor_low, index_i * BS, BS, 0)
    model = lax.dot_general(
        block_a, panel, (((1,), (1,)), ((), ())), preferred_element_type=jnp.float32
    )
    ratio = (block_counts.astype(jnp.float32) / model).astype(jnp.bfloat16)
    part = jnp.dot(ratio, panel, preferred_element_type=jnp.float32) * weight
    old = lax.dynamic_slice_in_dim(phi, index_i * BS, BS, 0)
    return lax.dynamic_update_slice_in_dim(phi, old + part, index_i * BS, 0)


def local(block_coords, live_blocks, counts, factor_a, factor_b, factor_c):
    coords = block_coords.reshape(SLOTS, 3)
    local_counts = counts.reshape(SLOTS, BS, BS * BS)
    weights = (jnp.arange(SLOTS, dtype=jnp.int32) < live_blocks.reshape(())).astype(jnp.float32)
    rows_b = collect(factor_b, "ka", 0)
    rows_c = collect(factor_c, "ia", 1)
    sums_b = rows_b.reshape(RB2, BS, R).sum(axis=1)
    sums_c = rows_c.reshape(RB3, BS, R).sum(axis=1)
    pick_j = (coords[:, 1:2] == jnp.arange(RB2, dtype=jnp.int32)[None, :]).astype(jnp.float32)
    pick_k = (coords[:, 2:3] == jnp.arange(RB3, dtype=jnp.int32)[None, :]).astype(jnp.float32)
    masses = jnp.dot(pick_j, sums_b, precision=lax.Precision.HIGHEST) * jnp.dot(
        pick_k, sums_c, precision=lax.Precision.HIGHEST
    )
    pick_i = (coords[:, 0:1] == jnp.arange(RB1, dtype=jnp.int32)[None, :]).astype(
        jnp.float32
    ) * weights[:, None]
    mass_part = lax.dot_general(
        pick_i, masses, (((0,), (0,)), ((), ())), precision=lax.Precision.HIGHEST
    )
    mass = over_copies(mass_part, ("ja", "ka"))
    mass_rows = jnp.broadcast_to(mass[:, None, :], (RB1, BS, R)).reshape(RB1 * BS, R)
    owned = factor_a.shape[0]
    first_row = lax.axis_index(("ja", "ka")) * owned
    my_mass = lax.dynamic_slice_in_dim(mass_rows, first_row, owned, 0)
    empty = jnp.zeros((RB1 * BS, R), jnp.float32)
    panels = jax.vmap(lambda index_j, index_k: make_panel(rows_b, rows_c, index_j, index_k))(
        coords[:, 1], coords[:, 2]
    )
    current = factor_a
    for turn in range(2):
        whole = collect(current.astype(jnp.bfloat16), ("ja", "ka"), 0)
        factor_low = whole

        def step(phi, item):
            index_i, weight, block_counts, panel = item
            return (add_block(phi, factor_low, panel, index_i, weight, block_counts), None)

        phi, _ = lax.scan(step, empty, (coords[:, 0], weights, local_counts, panels))
        mine = sent_and_summed(phi, ("ja", "ka"), 0)
        current = current * mine / my_mass
    return current


def solution(mesh):
    placed = (
        P("ia", "ja", "ka", None, None),
        P("ia", "ja", "ka"),
        P("ia", "ja", "ka", None, None, None),
        P(("ia", "ja", "ka"), None),
        P(("ja", "ka"), None),
        P("ka", "ia"),
    )
    return jax.shard_map(
        local, mesh=mesh, in_specs=placed, out_specs=P(("ia", "ja", "ka"), None), check_vma=False
    )
```

profile of v0, /device:TPU:6, one launch (start us, length us, event | category | flops | bytes accessed | tf_op | source)
XLA Modules:
  0.0 215.9 jit_solution(1743367901844112929)
XLA Ops:
  0.0 1.5 broadcast_in_dim.17
  1.5 4.5 %all-to-all-start.2 = ((f32[8,256,32]{1,2,0:T(8,128)}), f32[8,256,32]{1,2,0:T(8,128)S(1)}, u32[]{:S(2)}, u32[]{:S(2)}) async-start(f32[8,256,32]{1,2,0:T(8,128)} %broadcast_in_dim.17), calls=%async_computation.2 | async-start | bytes 524288 | tf_op jit(solution)/shard_map/all_to_all | solution.py:16
  5.9 0.7 convert_element_type.40
  6.6 6.8 %all-to-all-done.2 = f32[8,256,32]{1,2,0:T(8,128)S(1)} async-done(((f32[8,256,32]{1,2,0:T(8,128)}), f32[8,256,32]{1,2,0:T(8,128)S(1)}, u32[]{:S(2)}, u32[]{:S(2)}) %all-to-all-start.2) | async-done | bytes 262176 | tf_op jit(solution)/shard_map/all_to_all | solution.py:16
  13.4 0.7 broadcast_in_dim.15
  14.1 18.8 %all-to-all-start = ((bf16[64,4,256]{2,1,0:T(4,128)(2,1)}), bf16[64,4,256]{2,1,0:T(4,128)(2,1)S(1)}, u32[]{:S(2)}, u32[]{:S(2)}) async-start(bf16[64,4,256]{2,1,0:T(4,128)(2,1)} %broadcast_in_dim.15), calls=%async_computation | async-start | bytes 262144 | tf_op jit(solution)/shard_map/all_to_all | solution.py:16
  32.9 0.8 copy.28
  34.5 13.5 %all-to-all-done = bf16[64,4,256]{2,1,0:T(4,128)(2,1)S(1)} async-done(((bf16[64,4,256]{2,1,0:T(4,128)(2,1)}), bf16[64,4,256]{2,1,0:T(4,128)(2,1)S(1)}, u32[]{:S(2)}, u32[]{:S(2)}) %all-to-all-start) | async-done | bytes 131104 | tf_op jit(solution)/shard_map/all_to_all | solution.py:16
  48.0 1.5 broadcast_in_dim.16
  49.5 3.4 %all-to-all-start.1 = ((f32[8,32,256]{2,1,0:T(8,128)}), f32[8,32,256]{2,1,0:T(8,128)S(1)}, u32[]{:S(2)}, u32[]{:S(2)}) async-start(f32[8,32,256]{2,1,0:T(8,128)} %broadcast_in_dim.16), calls=%async_computation.1 | async-start | bytes 524288 | tf_op jit(solution)/shard_map/all_to_all | solution.py:16
  54.1 14.2 %all-to-all-done.1 = f32[8,32,256]{2,1,0:T(8,128)S(1)} async-done(((f32[8,32,256]{2,1,0:T(8,128)}), f32[8,32,256]{2,1,0:T(8,128)S(1)}, u32[]{:S(2)}, u32[]{:S(2)}) %all-to-all-start.1) | async-done | bytes 262176 | tf_op jit(solution)/shard_map/all_to_all | solution.py:16
  69.0 0.8 broadcast_in_dim.36
  69.8 11.3 %all-to-all-start.4 = ((f32[64,4,256]{2,1,0:T(4,128)}), f32[64,4,256]{2,1,0:T(4,128)S(1)}, u32[]{:S(2)}, u32[]{:S(2)}) async-start(f32[64,4,256]{2,1,0:T(4,128)} %broadcast_in_dim.36), calls=%async_computation.4 | async-start | bytes 524288 | tf_op jit(solution)/shard_map/all_to_all | solution.py:16
  81.4 7.0 %multiply_convert_fusion = bf16[4,64,64,256]{3,2,1,0:T(8,128)(2,1)} fusion(f32[4,64,256]{2,1,0:T(8,128)S(1)} %get-tuple-element.96, f32[4,64,256]{2,1,0:T(8,128)S(1)} %get-tuple-element.88), kind=kLoop, calls=%fused_computation.28 | loop fusion | flops 8388608 | bytes 8912896 | tf_op jit(solution)/shard_map/vmap()/convert_element_type | solution.py:49
  88.5 24.9 %while.22 = (s32[]{:T(128)}, f32[256,256]{1,0:T(8,128)S(1)}, s32[4]{0:T(128)S(1)}, s32[4,64,4096]{2,1,0:T(8,128)}, bf16[256,256]{1,0:T(8,128)(2,1)S(1)}, /*index...) while((s32[]{:T(128)}, f32[256,256]{1,0:T(8,128)S(1)}, ...), condition=%wide.region_1.0_spmd, body=%wide.region_0.0_spmd.sunk | while | flops 269254656 | bytes 5409979 | solution.py:100
  90.3 4.4 %fusion.66 = f32[256,256]{1,0:T(8,128)S(1)} fusion(f32[256,256]{1,0:T(8,128)S(1)} %get-tuple-element.377, s32[]{:T(128)S(6)} %select_n.28, bf16[4,4096,256]{2,1,0:T(8,128)(2,1)} %get-tuple-element.392, s32[]{:T(128)S(6)} %copy.58, s32[4,64,4096]{2,1,0:T(8,128)} %get-tuple-element.390, f32[]{:T(128)} %bitcast.84, ...), kind=kOutput, calls=%fused_computation.9.clone.1 | convolution fusion | flops 269254656 | bytes 5409792 | tf_op jit(solution)/shard_map/while/body/eval_jaxpr/dot_general | solution.py:58
  96.6 4.4 %fusion.66 = f32[256,256]{1,0:T(8,128)S(1)} fusion(f32[256,256]{1,0:T(8,128)S(1)} %get-tuple-element.377, s32[]{:T(128)S(6)} %select_n.28, bf16[4,4096,256]{2,1,0:T(8,128)(2,1)} %get-tuple-element.392, s32[]{:T(128)S(6)} %copy.58, s32[4,64,4096]{2,1,0:T(8,128)} %get-tuple-element.390, f32[]{:T(128)} %bitcast.84, ...), kind=kOutput, calls=%fused_computation.9.clone.1 | convolution fusion | flops 269254656 | bytes 5409792 | tf_op jit(solution)/shard_map/while/body/eval_jaxpr/dot_general | solution.py:58
  102.8 4.4 %fusion.66 = f32[256,256]{1,0:T(8,128)S(1)} fusion(f32[256,256]{1,0:T(8,128)S(1)} %get-tuple-element.377, s32[]{:T(128)S(6)} %select_n.28, bf16[4,4096,256]{2,1,0:T(8,128)(2,1)} %get-tuple-element.392, s32[]{:T(128)S(6)} %copy.58, s32[4,64,4096]{2,1,0:T(8,128)} %get-tuple-element.390, f32[]{:T(128)} %bitcast.84, ...), kind=kOutput, calls=%fused_computation.9.clone.1 | convolution fusion | flops 269254656 | bytes 5409792 | tf_op jit(solution)/shard_map/while/body/eval_jaxpr/dot_general | solution.py:58
  109.0 4.4 %fusion.66 = f32[256,256]{1,0:T(8,128)S(1)} fusion(f32[256,256]{1,0:T(8,128)S(1)} %get-tuple-element.377, s32[]{:T(128)S(6)} %select_n.28, bf16[4,4096,256]{2,1,0:T(8,128)(2,1)} %get-tuple-element.392, s32[]{:T(128)S(6)} %copy.58, s32[4,64,4096]{2,1,0:T(8,128)} %get-tuple-element.390, f32[]{:T(128)} %bitcast.84, ...), kind=kOutput, calls=%fused_computation.9.clone.1 | convolution fusion | flops 269254656 | bytes 5409792 | tf_op jit(solution)/shard_map/while/body/eval_jaxpr/dot_general | solution.py:58
  113.4 0.8 reshape.56
  114.1 15.1 %all-to-all-start.3 = ((f32[64,4,256]{2,1,0:T(4,128)}), f32[64,4,256]{2,1,0:T(4,128)S(1)}, u32[]{:S(2)}, u32[]{:S(2)}) async-start(f32[64,4,256]{2,1,0:T(4,128)} %reshape.56), calls=%async_computation.3 | async-start | bytes 524288 | tf_op jit(solution)/shard_map/all_to_all | solution.py:42
  129.4 16.9 %all-to-all-done.3 = f32[64,4,256]{2,1,0:T(4,128)S(1)} async-done(((f32[64,4,256]{2,1,0:T(4,128)}), f32[64,4,256]{2,1,0:T(4,128)S(1)}, u32[]{:S(2)}, u32[]{:S(2)}) %all-to-all-start.3) | async-done | bytes 262176 | tf_op jit(solution)/shard_map/all_to_all | solution.py:42
  146.4 0.7 broadcast_in_dim.38
  147.1 6.7 %all-to-all-start.5 = ((bf16[64,4,256]{2,1,0:T(4,128)(2,1)}), bf16[64,4,256]{2,1,0:T(4,128)(2,1)S(1)}, u32[]{:S(2)}, u32[]{:S(2)}) async-start(bf16[64,4,256]{2,1,0:T(4,128)(2,1)} %broadcast_in_dim.38), calls=%async_computation.5 | async-start | bytes 262144 | tf_op jit(solution)/shard_map/all_to_all | solution.py:16
  153.9 14.3 %all-to-all-done.5 = bf16[64,4,256]{2,1,0:T(4,128)(2,1)S(1)} async-done(((bf16[64,4,256]{2,1,0:T(4,128)(2,1)}), bf16[64,4,256]{2,1,0:T(4,128)(2,1)S(1)}, u32[]{:S(2)}, u32[]{:S(2)}) %all-to-all-start.5) | async-done | bytes 131104 | tf_op jit(solution)/shard_map/all_to_all | solution.py:16
  168.2 24.1 %while.23 = (s32[]{:T(128)}, f32[256,256]{1,0:T(8,128)S(1)}, s32[4]{0:T(128)S(1)}, s32[4,64,4096]{2,1,0:T(8,128)}, bf16[256,256]{1,0:T(8,128)(2,1)S(1)}, /*index...) while((s32[]{:T(128)}, f32[256,256]{1,0:T(8,128)S(1)}, ...), condition=%wide.region_8.9_spmd, body=%wide.region_7.8_spmd.sunk | while | flops 269254656 | bytes 5409979 | solution.py:100
  169.9 4.3 %fusion.70 = f32[256,256]{1,0:T(8,128)S(1)} fusion(f32[256,256]{1,0:T(8,128)S(1)} %get-tuple-element.410, s32[]{:T(128)S(6)} %select_n.29, bf16[4,4096,256]{2,1,0:T(8,128)(2,1)} %get-tuple-element.425, s32[]{:T(128)S(6)} %copy.64, s32[4,64,4096]{2,1,0:T(8,128)} %get-tuple-element.423, f32[]{:T(128)} %bitcast.89, ...), kind=kOutput, calls=%fused_computation.21.clone.1 | convolution fusion | flops 269254656 | bytes 5409792 | tf_op jit(solution)/shard_map/while/body/eval_jaxpr/dot_general | solution.py:58
  175.9 4.3 %fusion.70 = f32[256,256]{1,0:T(8,128)S(1)} fusion(f32[256,256]{1,0:T(8,128)S(1)} %get-tuple-element.410, s32[]{:T(128)S(6)} %select_n.29, bf16[4,4096,256]{2,1,0:T(8,128)(2,1)} %get-tuple-element.425, s32[]{:T(128)S(6)} %copy.64, s32[4,64,4096]{2,1,0:T(8,128)} %get-tuple-element.423, f32[]{:T(128)} %bitcast.89, ...), kind=kOutput, calls=%fused_computation.21.clone.1 | convolution fusion | flops 269254656 | bytes 5409792 | tf_op jit(solution)/shard_map/while/body/eval_jaxpr/dot_general | solution.py:58
  182.0 4.3 %fusion.70 = f32[256,256]{1,0:T(8,128)S(1)} fusion(f32[256,256]{1,0:T(8,128)S(1)} %get-tuple-element.410, s32[]{:T(128)S(6)} %select_n.29, bf16[4,4096,256]{2,1,0:T(8,128)(2,1)} %get-tuple-element.425, s32[]{:T(128)S(6)} %copy.64, s32[4,64,4096]{2,1,0:T(8,128)} %get-tuple-element.423, f32[]{:T(128)} %bitcast.89, ...), kind=kOutput, calls=%fused_computation.21.clone.1 | convolution fusion | flops 269254656 | bytes 5409792 | tf_op jit(solution)/shard_map/while/body/eval_jaxpr/dot_general | solution.py:58
  188.0 4.3 %fusion.70 = f32[256,256]{1,0:T(8,128)S(1)} fusion(f32[256,256]{1,0:T(8,128)S(1)} %get-tuple-element.410, s32[]{:T(128)S(6)} %select_n.29, bf16[4,4096,256]{2,1,0:T(8,128)(2,1)} %get-tuple-element.425, s32[]{:T(128)S(6)} %copy.64, s32[4,64,4096]{2,1,0:T(8,128)} %get-tuple-element.423, f32[]{:T(128)} %bitcast.89, ...), kind=kOutput, calls=%fused_computation.21.clone.1 | convolution fusion | flops 269254656 | bytes 5409792 | tf_op jit(solution)/shard_map/while/body/eval_jaxpr/dot_general | solution.py:58
  192.4 22.8 %all_to_all.35 = f32[64,4,256]{2,1,0:T(4,128)S(1)} all-to-all(f32[64,4,256]{2,1,0:T(4,128)S(1)} %reshape.59), channel_id=1, replica_groups=mesh['ia'=8,'ja'=8,'ka'=8] {'ja','ka'}, dimensions={0} | all-to-all | bytes 524288 | tf_op jit(solution)/shard_map/all_to_all | solution.py:42
  215.3 0.6 multiply_divide_fusion
  (62 shorter events, 12.6 us)
Async XLA Ops:
  1.5 12.0 %all-to-all-start.2 = ((f32[8,256,32]{1,2,0:T(8,128)}), f32[8,256,32]{1,2,0:T(8,128)S(1)}, u32[]{:S(2)}, u32[]{:S(2)}) async-start(f32[8,256,32]{1,2,0:T(8,128)} %broadcast_in_dim.17), calls=%async_computation.2 | async-start | bytes 524288 | tf_op jit(solution)/shard_map/all_to_all | solution.py:16
  14.1 33.9 %all-to-all-start = ((bf16[64,4,256]{2,1,0:T(4,128)(2,1)}), bf16[64,4,256]{2,1,0:T(4,128)(2,1)S(1)}, u32[]{:S(2)}, u32[]{:S(2)}) async-start(bf16[64,4,256]{2,1,0:T(4,128)(2,1)} %broadcast_in_dim.15), calls=%async_computation | async-start | bytes 262144 | tf_op jit(solution)/shard_map/all_to_all | solution.py:16
  49.5 18.8 %all-to-all-start.1 = ((f32[8,32,256]{2,1,0:T(8,128)}), f32[8,32,256]{2,1,0:T(8,128)S(1)}, u32[]{:S(2)}, u32[]{:S(2)}) async-start(f32[8,32,256]{2,1,0:T(8,128)} %broadcast_in_dim.16), calls=%async_computation.1 | async-start | bytes 524288 | tf_op jit(solution)/shard_map/all_to_all | solution.py:16
  69.8 44.4 %all-to-all-start.4 = ((f32[64,4,256]{2,1,0:T(4,128)}), f32[64,4,256]{2,1,0:T(4,128)S(1)}, u32[]{:S(2)}, u32[]{:S(2)}) async-start(f32[64,4,256]{2,1,0:T(4,128)} %broadcast_in_dim.36), calls=%async_computation.4 | async-start | bytes 524288 | tf_op jit(solution)/shard_map/all_to_all | solution.py:16
  88.5 57.9 %copy-start = (f32[4,256]{1,0:T(4,128)S(1)}, f32[4,256]{1,0:T(4,128)}, u32[]{:S(2)}) copy-start(f32[4,256]{1,0:T(4,128)} %param.13) | copy-start | bytes 12292
  114.1 32.1 %all-to-all-start.3 = ((f32[64,4,256]{2,1,0:T(4,128)}), f32[64,4,256]{2,1,0:T(4,128)S(1)}, u32[]{:S(2)}, u32[]{:S(2)}) async-start(f32[64,4,256]{2,1,0:T(4,128)} %reshape.56), calls=%async_computation.3 | async-start | bytes 524288 | tf_op jit(solution)/shard_map/all_to_all | solution.py:42
  147.1 21.0 %all-to-all-start.5 = ((bf16[64,4,256]{2,1,0:T(4,128)(2,1)}), bf16[64,4,256]{2,1,0:T(4,128)(2,1)S(1)}, u32[]{:S(2)}, u32[]{:S(2)}) async-start(bf16[64,4,256]{2,1,0:T(4,128)(2,1)} %broadcast_in_dim.38), calls=%async_computation.5 | async-start | bytes 262144 | tf_op jit(solution)/shard_map/all_to_all | solution.py:16
where the time goes:
time: 217 us; the launch traced here: 216 us
  waiting for transfers between devices  65.6 us (30%)
  starting transfers between devices  59.8 us (28%)
  matrix products  35.3 us (16%)
  blocking collectives  22.8 us (11%)
  local copies, waits for them, and re-layouts  17 us (8%)
  other arithmetic  9.2 us (4%)
  loops' own time  5.26 us (2%)
    all_to_all x5, waiting for transfers between devices, from_everyone(): return lax.all_to_all(copies, axis, split_axis=0, concat_axis=0, tiled=True)  48.7 us
    all_to_all x5, starting transfers between devices, from_everyone(): return lax.all_to_all(copies, axis, split_axis=0, concat_axis=0, tiled=True)  44.7 us
    dot_general x8, matrix products, add_block(): part = jnp.dot(ratio, panel, preferred_element_type=jnp.float32) * weight  34.6 us
    all_to_all x1, blocking collectives, sent_and_summed(): lax.all_to_all(blocks, axis, split_axis=0, concat_axis=0, tiled=True)  22.8 us
    all_to_all x1, waiting for transfers between devices, sent_and_summed(): lax.all_to_all(blocks, axis, split_axis=0, concat_axis=0, tiled=True)  16.9 us
    all_to_all x1, starting transfers between devices, sent_and_summed(): lax.all_to_all(blocks, axis, split_axis=0, concat_axis=0, tiled=True)  15.1 us
    dynamic_slice x16, local copies, waits for them, and re-layouts, local(): lax.scan(step, empty, (coords[:, 0], weights, local_counts, panels))  9.31 us
    convert_element_type x1, other arithmetic, make_panel(): (piece_b[:, None, :] * piece_c[None, :, :]).reshape(BS * BS, R)  7.04 us
  transfers between devices with their start and end apart: 6, of which 5 were waited for; matrix products, arithmetic and copies ran while one was open for 15% of the time, Pallas kernels for 0%

commit v1 on v0

v1 whole, which is shorter than its diff:
```python
import jax
import jax.numpy as jnp
from jax import lax
from jax.experimental import pallas as pl
from jax.experimental.pallas import tpu as pltpu
from jax.sharding import Mesh, PartitionSpec as P

R = 256
BS = 64
RB1 = 4
SLOTS = 4
SPAN = 1024
F32 = jnp.float32
BF16 = jnp.bfloat16

IA = "ia"
JX = "jx"
JZ = "jz"
KA = "ka"
JK = (JX, JZ, KA)
ZK = (JZ, KA)


def swap(x, axis):
    return lax.all_to_all(x, axis, split_axis=0, concat_axis=0, tiled=True)


def from_everyone(x, axis):
    return swap(jnp.broadcast_to(x, (lax.axis_size(axis), *x.shape)), axis)


def aligned(start, size):
    return pl.ds(pl.multiple_of(start * size, size), size)


def block_order(eighth, half):
    return half * 8 + eighth


def prep_kernel(coords, live, both, rows_c, mass):
    rows_c[...] = jnp.swapaxes(both[:, 32:, :].reshape(R, R), 0, 1)
    mass[...] = jnp.zeros_like(mass)
    for slot in range(SLOTS):

        @pl.when(slot < live[0])
        def _():
            g = coords[slot * 3]
            j = coords[slot * 3 + 1]
            k = coords[slot * 3 + 2]
            piece_b = both[:, aligned(j, 8), :].reshape(BS, R)
            piece_c = rows_c[aligned(k, BS), :]
            sum_b = jnp.sum(piece_b, axis=0, keepdims=True)
            sum_c = jnp.sum(piece_c, axis=0, keepdims=True)
            mass[g, 0:1, :] = mass[g, 0:1, :] + sum_b * sum_c


def prepare(coords, live, both):
    return pl.pallas_call(
        prep_kernel,
        grid_spec=pltpu.PrefetchScalarGridSpec(
            num_scalar_prefetch=2,
            grid=(1,),
            in_specs=[pl.BlockSpec((8, 64, R), lambda s, *_: (0, 0, 0))],
            out_specs=[
                pl.BlockSpec((R, R), lambda s, *_: (0, 0)),
                pl.BlockSpec((RB1, 8, R), lambda s, *_: (0, 0, 0)),
            ],
        ),
        out_shape=[
            jax.ShapeDtypeStruct((R, R), F32),
            jax.ShapeDtypeStruct((RB1, 8, R), F32),
        ],
        name="prepare",
    )(coords, live, both)


def pass_kernel(with_mass):
    def kernel(coords, live, counts, factor, both, rows_c, *rest):
        if with_mass:
            mass, out, panel = rest
        else:
            out, panel = rest
        slot = pl.program_id(0)

        @pl.when(slot == 0)
        def _():
            out[:, :BS, :] = jnp.zeros((RB1, BS, R), F32)
            if with_mass:
                out[:, BS:, :] = mass[...]

        @pl.when(slot < live[0])
        def _():
            i = coords[slot * 3]
            j = coords[slot * 3 + 1]
            k = coords[slot * 3 + 2]
            piece_a = factor[aligned(i, BS), :]
            piece_c = rows_c[aligned(k, BS), :]
            for half in range(2):
                for eighth in range(8):
                    rows_b = both[eighth, aligned(j, 8), :]
                    first = block_order(eighth, half) * 4
                    for q in range(4):
                        row = rows_b[half * 4 + q : half * 4 + q + 1, :]
                        panel[(first + q) * BS : (first + q + 1) * BS, :] = (
                            row * piece_c
                        ).astype(BF16)
            total = jnp.zeros((BS, R), F32)
            for start in range(0, BS * BS, SPAN):
                piece = panel[start : start + SPAN, :]
                model = lax.dot_general(
                    piece_a, piece, (((1,), (1,)), ((), ())), preferred_element_type=F32
                )
                hits = counts[0, :, start : start + SPAN].astype(F32)
                ratio = (hits / model).astype(BF16)
                total = total + jnp.dot(ratio, piece, preferred_element_type=F32)
            out[i, :BS, :] = out[i, :BS, :] + total

    return kernel


def run_pass(coords, live, counts, factor, both, rows_c, mass=None):
    rows = BS if mass is None else BS + 8
    in_specs = [
        pl.BlockSpec((1, BS, BS * BS), lambda s, *_: (s, 0, 0)),
        pl.BlockSpec((R, R), lambda s, *_: (0, 0)),
        pl.BlockSpec((8, 64, R), lambda s, *_: (0, 0, 0)),
        pl.BlockSpec((R, R), lambda s, *_: (0, 0)),
    ]
    args = [counts, factor, both, rows_c]
    if mass is not None:
        in_specs.append(pl.BlockSpec((RB1, 8, R), lambda s, *_: (0, 0, 0)))
        args.append(mass)
    return pl.pallas_call(
        pass_kernel(mass is not None),
        grid_spec=pltpu.PrefetchScalarGridSpec(
            num_scalar_prefetch=2,
            grid=(SLOTS,),
            in_specs=in_specs,
            out_specs=pl.BlockSpec((RB1, rows, R), lambda s, *_: (0, 0, 0)),
            scratch_shapes=[pltpu.VMEM((BS * BS, R), BF16)],
        ),
        out_shape=jax.ShapeDtypeStruct((RB1, rows, R), F32),
        compiler_params=pltpu.CompilerParams(dimension_semantics=("arbitrary",)),
        name="one_pass",
    )(coords, live, *args)


def local(block_coords, live_blocks, counts, factor_a, factor_b, factor_c):
    coords = block_coords.reshape(SLOTS * 3)
    live = live_blocks.reshape(1)
    hits = counts.reshape(SLOTS, BS, BS * BS)
    mine_b = lax.dynamic_slice_in_dim(factor_b, lax.axis_index(IA) * 4, 4, 0)
    share_b = from_everyone(mine_b, KA).reshape(32, R)
    both = from_everyone(jnp.concatenate([share_b, factor_c.T], axis=0), IA)
    low = from_everyone(factor_a.astype(BF16), JK).reshape(R, R)
    rows_c, mass = prepare(coords, live, both)

    phi = run_pass(coords, live, hits, low, both, rows_c, mass)
    part = swap(phi, JX).sum(axis=0)
    rows = jnp.concatenate(
        [part[:BS].reshape(16, 4, R), jnp.broadcast_to(part[BS:, :][None, :4], (16, 4, R))], axis=1
    )
    mine = swap(rows, ZK).sum(axis=0)
    my_mass = mine[4:5]
    first = factor_a * mine[:4] / my_mass
    low = from_everyone(first.astype(BF16), JK).reshape(R, R)
    phi = run_pass(coords, live, hits, low, both, rows_c)
    part = swap(phi, JX).sum(axis=0)
    mine = swap(part.reshape(16, 4, R), ZK).sum(axis=0)
    return first * mine / my_mass


def solution(mesh):
    shape = mesh.shape
    fine = Mesh(
        mesh.devices.reshape(shape["ia"], shape["ja"] // 2, 2, shape["ka"]), (IA, JX, JZ, KA)
    )
    placed = (
        P(IA, (JX, JZ), KA, None, None),
        P(IA, (JX, JZ), KA),
        P(IA, (JX, JZ), KA, None, None, None),
        P((IA, JX, JZ, KA), None),
        P((JX, JZ, KA), None),
        P(KA, IA),
    )
    return jax.shard_map(
        local, mesh=fine, in_specs=placed, out_specs=P((IA, JX, JZ, KA), None), check_vma=False
    )
```

time: 217 us -> 162 us (0.75)
  blocking collectives: 22.8 us -> 76.9 us
  matrix products: 35.3 us -> 0 us
  waiting for transfers between devices: 65.6 us -> 30.8 us
  starting transfers between devices: 59.8 us -> 28.3 us
  Pallas kernels: 0 us -> 15.6 us
  local copies, waits for them, and re-layouts: 17 us -> 6.52 us
  other arithmetic: 9.2 us -> 2.19 us
  loops' own time: 5.26 us -> 0 us
    all_to_all x1 -> x5, blocking collectives: 22.8 us -> 76.9 us  [swap(): return lax.all_to_all(x, axis, split_axis=0, concat_axis=0, tiled=True)]
    dot_general x11 -> x0, matrix products: 35.3 us -> none  [the longest x8 34.6 us: add_block(): part = jnp.dot(ratio, panel, preferred_element_type=jnp.float32) * weight]
    all_to_all x6 -> x3, waiting for transfers between devices: 65.6 us -> 30.8 us  [swap(): return lax.all_to_all(x, axis, split_axis=0, concat_axis=0, tiled=True)]
    all_to_all x6 -> x3, starting transfers between devices: 59.8 us -> 28.3 us  [swap(): return lax.all_to_all(x, axis, split_axis=0, concat_axis=0, tiled=True)]
    pallas_call x0 -> x3, Pallas kernels: none -> 15.6 us  [the longest x2 13 us: run_pass(): pl.pallas_call(pass_kernel(mass is not None), grid_spec=pltpu.PrefetchSca...]
    dynamic_slice x16 -> x1, local copies, waits for them, and re-layouts: 9.31 us -> 0.01 us  [local(): mine_b = lax.dynamic_slice_in_dim(factor_b, lax.axis_index(IA) * 4, 4, 0)]
    convert_element_type x4 -> x2, other arithmetic: 7.75 us -> 0.7 us  [the longest x1 0.69 us: local(): low = from_everyone(factor_a.astype(BF16), JK).reshape(R, R)]
    another operation x4 -> x0, loops' own time: 5.26 us -> none  [the longest x2 5.03 us: local(): lax.scan(step, empty, (coords[:, 0], weights, local_counts, panels))]
  transfers between devices with their start and end apart: 6 -> 3, of which waited for: 5 -> 3; matrix products, arithmetic and copies ran while one was open for 15% -> 2% of each run, Pallas kernels for 0% -> 0%
where the time goes in v1:
time: 162 us; the launch traced here: 161 us
  blocking collectives  76.9 us (47%)
  waiting for transfers between devices  30.8 us (19%)
  starting transfers between devices  28.3 us (17%)
  Pallas kernels  15.6 us (10%)
  local copies, waits for them, and re-layouts  6.52 us (4%)
  other arithmetic  2.19 us (1%)
    all_to_all x5, blocking collectives, swap(): return lax.all_to_all(x, axis, split_axis=0, concat_axis=0, tiled=True)  76.9 us
    all_to_all x3, waiting for transfers between devices, swap(): return lax.all_to_all(x, axis, split_axis=0, concat_axis=0, tiled=True)  30.8 us
    all_to_all x3, starting transfers between devices, swap(): return lax.all_to_all(x, axis, split_axis=0, concat_axis=0, tiled=True)  28.3 us
    pallas_call x2, Pallas kernels, run_pass(): pl.pallas_call(pass_kernel(mass is not None), grid_spec=pltpu.PrefetchSca...  13 us
  transfers between devices with their start and end apart: 3, of which 3 were waited for; matrix products, arithmetic and copies ran while one was open for 2% of the time, Pallas kernels for 0%

profile of v1, /device:TPU:6, one launch (start us, length us, event | category | flops | bytes accessed | tf_op | source)
XLA Modules:
  0.0 161.0 jit_solution(14643676501976559998)
XLA Ops:
  0.0 0.0 copy-start
  0.0 0.8 copy-done
  0.8 0.6 broadcast_in_dim.19
  1.4 12.5 %all-to-all-start.1 = ((f32[8,4,256]{2,1,0:T(4,128)}), f32[8,4,256]{2,1,0:T(4,128)S(1)}, u32[]{:S(2)}, u32[]{:S(2)}) async-start(f32[8,4,256]{2,1,0:T(4,128)} %broadcast_in_dim.19), calls=%async_computation.1 | async-start | bytes 65536 | tf_op jit(solution)/shard_map/all_to_all | solution.py:25
  13.9 0.7 convert_element_type.6
  14.6 9.9 %all-to-all-done.1 = f32[8,4,256]{2,1,0:T(4,128)S(1)} async-done(((f32[8,4,256]{2,1,0:T(4,128)}), f32[8,4,256]{2,1,0:T(4,128)S(1)}, u32[]{:S(2)}, u32[]{:S(2)}) %all-to-all-start.1) | async-done | bytes 32800 | tf_op jit(solution)/shard_map/all_to_all | solution.py:25
  24.5 0.7 broadcast_in_dim.18
  25.2 11.3 %all-to-all-start = ((bf16[64,4,256]{2,1,0:T(4,128)(2,1)}), bf16[64,4,256]{2,1,0:T(4,128)(2,1)S(1)}, u32[]{:S(2)}, u32[]{:S(2)}) async-start(bf16[64,4,256]{2,1,0:T(4,128)(2,1)} %broadcast_in_dim.18), calls=%async_computation | async-start | bytes 262144 | tf_op jit(solution)/shard_map/all_to_all | solution.py:25
  36.5 0.8 pad_maximum_fusion.1
  37.3 13.3 %all-to-all-done = bf16[64,4,256]{2,1,0:T(4,128)(2,1)S(1)} async-done(((bf16[64,4,256]{2,1,0:T(4,128)(2,1)}), bf16[64,4,256]{2,1,0:T(4,128)(2,1)S(1)}, u32[]{:S(2)}, u32[]{:S(2)}) %all-to-all-start) | async-done | bytes 131104 | tf_op jit(solution)/shard_map/all_to_all | solution.py:25
  50.6 0.8 broadcast_in_dim.20
  51.4 4.5 %all-to-all-start.2 = ((f32[8,64,256]{2,1,0:T(8,128)}), f32[8,64,256]{2,1,0:T(8,128)S(1)}, u32[]{:S(2)}, u32[]{:S(2)}) async-start(f32[8,64,256]{2,1,0:T(8,128)} %broadcast_in_dim.20), calls=%async_computation.2 | async-start | bytes 1048576 | tf_op jit(solution)/shard_map/all_to_all | solution.py:25
  55.9 0.0 copy-start.2
  56.5 0.8 copy.10
  57.3 0.6 reshape.25.coords
  57.9 0.7 reshape.28.factor
  58.6 7.6 %all-to-all-done.2.both = f32[8,64,256]{2,1,0:T(8,128)S(1)} async-done(((f32[8,64,256]{2,1,0:T(8,128)}), f32[8,64,256]{2,1,0:T(8,128)S(1)}, u32[]{:S(2)}, u32[]{:S(2)}) %all-to-all-start.2) | async-done | bytes 524320 | tf_op jit(solution)/shard_map/all_to_all | solution.py:25
  66.2 0.0 copy-start.1
  66.2 0.8 copy-done.1
  67.0 2.6 %prepare.1 = (f32[256,256]{1,0:T(8,128)}, f32[4,8,256]{2,1,0:T(8,128)}) custom-call(s32[12]{0:T(128)} %reshape.25.coords, s32[1]{0:T(128)} %bitcast.4.live, f32[8,64,256]{2,1,0:T(8,128)} %copy-done.1), custom_call_target="tpu_custom_call" | custom-call | tf_op jit(solution)/shard_map/prepare/pallas_call | solution.py:58
  69.6 6.5 %one_pass.2 = f32[4,72,256]{2,1,0:T(8,128)} custom-call(s32[12]{0:T(128)} %reshape.25.coords, s32[1]{0:T(128)} %bitcast.5.live, s32[4,64,4096]{2,1,0:T(8,128)} %bitcast.7, bf16[256,256]{1,0:T(8,128)(2,1)} %reshape.28.factor, f32[8,64,256]{2,1,0:T(8,128)} %copy-done.1, f32[256,256]{1,0:T(8,128)} %get-tuple-element.7.rows_c, f32[4,8,256]{2,1,0:T(8,128)} %get-tuple-element.8.rest_0_), custom_call_target="tpu_custom_call" | custom-call | tf_op jit(solution)/shard_map/one_pass/pallas_call | solution.py:133
  76.1 9.3 %all_to_all.40 = f32[4,72,256]{2,1,0:T(8,128)S(1)} all-to-all(f32[4,72,256]{2,1,0:T(8,128)} %one_pass.2), channel_id=1, replica_groups=mesh['ia'=8,'jx'=4,'jz'=2,'ka'=8] {'jx'}, dimensions={0} | all-to-all | bytes 589824 | tf_op jit(solution)/shard_map/all_to_all | solution.py:25
  85.5 19.4 %all_to_all.41 = f32[16,8,256]{2,1,0:T(8,128)S(1)} all-to-all(f32[16,8,256]{2,1,0:T(8,128)S(1)} %pad_maximum_fusion), channel_id=1, replica_groups=mesh['ia'=8,'jx'=4,'jz'=2,'ka'=8] {'jz','ka'}, dimensions={0} | all-to-all | bytes 262144 | tf_op jit(solution)/shard_map/all_to_all | solution.py:25
  104.9 0.0 copy-done.2
  105.0 21.7 %all_to_all.42 = bf16[64,4,256]{2,1,0:T(4,128)(2,1)S(1)} all-to-all(bf16[64,4,256]{2,1,0:T(4,128)(2,1)S(1)} %broadcast_in_dim.22), channel_id=1, replica_groups=mesh['ia'=8,'jx'=4,'jz'=2,'ka'=8] {'jx','jz','ka'}, dimensions={0} | all-to-all | bytes 262144 | tf_op jit(solution)/shard_map/all_to_all | solution.py:25
  126.7 0.7 reshape.31.factor
  127.4 6.5 %one_pass.3 = f32[4,64,256]{2,1,0:T(8,128)} custom-call(s32[12]{0:T(128)} %reshape.25.coords, s32[1]{0:T(128)} %bitcast.6.live, s32[4,64,4096]{2,1,0:T(8,128)} %bitcast.8, bf16[256,256]{1,0:T(8,128)(2,1)} %reshape.31.factor, f32[8,64,256]{2,1,0:T(8,128)} %copy-done.1, f32[256,256]{1,0:T(8,128)} %get-tuple-element.7.rows_c), custom_call_target="tpu_custom_call" | custom-call | tf_op jit(solution)/shard_map/one_pass/pallas_call | solution.py:133
  133.9 9.1 %all_to_all.43 = f32[4,64,256]{2,1,0:T(8,128)S(1)} all-to-all(f32[4,64,256]{2,1,0:T(8,128)} %one_pass.3), channel_id=1, replica_groups=mesh['ia'=8,'jx'=4,'jz'=2,'ka'=8] {'jx'}, dimensions={0} | all-to-all | bytes 524288 | tf_op jit(solution)/shard_map/all_to_all | solution.py:25
  143.0 17.4 %all_to_all.44 = f32[16,4,256]{2,1,0:T(4,128)S(1)} all-to-all(f32[16,4,256]{2,1,0:T(4,128)S(1)} %reshape.32), channel_id=1, replica_groups=mesh['ia'=8,'jx'=4,'jz'=2,'ka'=8] {'jz','ka'}, dimensions={0} | all-to-all | bytes 131072 | tf_op jit(solution)/shard_map/all_to_all | solution.py:25
  160.4 0.6 multiply_divide_fusion
  (15 shorter events, 0.3 us)
Async XLA Ops:
  0.0 0.8 copy-start
  1.4 23.2 %all-to-all-start.1 = ((f32[8,4,256]{2,1,0:T(4,128)}), f32[8,4,256]{2,1,0:T(4,128)S(1)}, u32[]{:S(2)}, u32[]{:S(2)}) async-start(f32[8,4,256]{2,1,0:T(4,128)} %broadcast_in_dim.19), calls=%async_computation.1 | async-start | bytes 65536 | tf_op jit(solution)/shard_map/all_to_all | solution.py:25
  25.2 25.3 %all-to-all-start = ((bf16[64,4,256]{2,1,0:T(4,128)(2,1)}), bf16[64,4,256]{2,1,0:T(4,128)(2,1)S(1)}, u32[]{:S(2)}, u32[]{:S(2)}) async-start(bf16[64,4,256]{2,1,0:T(4,128)(2,1)} %broadcast_in_dim.18), calls=%async_computation | async-start | bytes 262144 | tf_op jit(solution)/shard_map/all_to_all | solution.py:25
  51.4 14.8 %all-to-all-start.2 = ((f32[8,64,256]{2,1,0:T(8,128)}), f32[8,64,256]{2,1,0:T(8,128)S(1)}, u32[]{:S(2)}, u32[]{:S(2)}) async-start(f32[8,64,256]{2,1,0:T(8,128)} %broadcast_in_dim.20), calls=%async_computation.2 | async-start | bytes 1048576 | tf_op jit(solution)/shard_map/all_to_all | solution.py:25
  55.9 49.0 %copy-start.2 = (f32[4,256]{1,0:T(4,128)S(1)}, f32[4,256]{1,0:T(4,128)}, u32[]{:S(2)}) copy-start(f32[4,256]{1,0:T(4,128)} %param.9) | copy-start | bytes 12292
  66.2 0.8 copy-start.1

commit v2 on v1

v2 whole, which is shorter than its diff:
```python
import jax
import jax.numpy as jnp
from jax import lax
from jax.experimental import pallas as pl
from jax.experimental.pallas import tpu as pltpu
from jax.sharding import Mesh, PartitionSpec as P


R = 256
BS = 64
RB1 = 4
SLOTS = 4
SPAN = 1024
F32 = jnp.float32
F16 = jnp.float16
PHI_SCALE = 0.25
MASS_SCALE = 1.0 / 32.0
BF16 = jnp.bfloat16

IA = "ia"
JX = "jx"
JZ = "jz"
KA = "ka"
JK = (JX, JZ, KA)
ZK = (JZ, KA)


def swap(x, axis):
    return lax.all_to_all(x, axis, split_axis=0, concat_axis=0, tiled=True)


def from_everyone(x, axis):
    return swap(jnp.broadcast_to(x, (lax.axis_size(axis), *x.shape)), axis)


def aligned(start, size):
    return pl.ds(pl.multiple_of(start * size, size), size)


def block_order(eighth, half):
    return half * 8 + eighth


def prep_kernel(coords, live, both, rows_c, mass):
    rows_c[...] = jnp.swapaxes(both[:, 32:, :].reshape(R, R), 0, 1)
    mass[...] = jnp.zeros_like(mass)
    for slot in range(SLOTS):

        @pl.when(slot < live[0])
        def _():
            g = coords[slot * 3]
            j = coords[slot * 3 + 1]
            k = coords[slot * 3 + 2]
            piece_b = both[:, aligned(j, 8), :].reshape(BS, R)
            piece_c = rows_c[aligned(k, BS), :]
            sum_b = jnp.sum(piece_b, axis=0, keepdims=True)
            sum_c = jnp.sum(piece_c, axis=0, keepdims=True)
            mass[g, 0:1, :] = mass[g, 0:1, :] + sum_b * sum_c


def prepare(coords, live, both):
    whole = pl.BlockSpec(memory_space=pltpu.VMEM)
    scalars = pl.BlockSpec(memory_space=pltpu.SMEM)
    return pl.pallas_call(
        prep_kernel,
        in_specs=[scalars, scalars, whole],
        out_specs=[whole, whole],
        out_shape=[
            jax.ShapeDtypeStruct((R, R), F32),
            jax.ShapeDtypeStruct((RB1, 8, R), F32),
        ],
        compiler_params=pltpu.CompilerParams(vmem_limit_bytes=8 << 20),
        name="prepare",
    )(coords, live, both)


def pass_kernel(coords, live, counts, factor, both, rows_c, out, panel, hits, arrived):
    def fetch(slot):
        return pltpu.make_async_copy(counts.at[slot], hits.at[slot], arrived.at[slot])

    for slot in range(SLOTS):

        @pl.when(slot < live[0])
        def _():
            fetch(slot).start()

    out[...] = jnp.zeros_like(out)

    def step(slot, carry):
        i = coords[slot * 3]
        j = coords[slot * 3 + 1]
        k = coords[slot * 3 + 2]
        piece_a = factor[aligned(i, BS), :]
        piece_c = rows_c[aligned(k, BS), :]
        for half in range(2):
            for eighth in range(8):
                rows_b = both[eighth, aligned(j, 8), :]
                first = block_order(eighth, half) * 4
                for q in range(4):
                    row = rows_b[half * 4 + q : half * 4 + q + 1, :]
                    panel[(first + q) * BS : (first + q + 1) * BS, :] = (
                        row * piece_c
                    ).astype(BF16)
        fetch(slot).wait()
        total = jnp.zeros((BS, R), F32)
        for start in range(0, BS * BS, SPAN):
            piece = panel[start : start + SPAN, :]
            model = lax.dot_general(
                piece_a, piece, (((1,), (1,)), ((), ())), preferred_element_type=F32
            )
            count = hits[slot, :, start : start + SPAN].astype(F32)
            ratio = (count / model).astype(BF16)
            total = total + jnp.dot(ratio, piece, preferred_element_type=F32)
        out[i] = out[i] + total * (piece_a.astype(F32) * PHI_SCALE)
        return carry

    lax.fori_loop(0, live[0], step, 0)


def run_pass(coords, live, counts, factor, both, rows_c):
    whole = pl.BlockSpec(memory_space=pltpu.VMEM)
    scalars = pl.BlockSpec(memory_space=pltpu.SMEM)
    return pl.pallas_call(
        pass_kernel,
        in_specs=[scalars, scalars, pl.BlockSpec(memory_space=pltpu.HBM), whole, whole, whole],
        out_specs=whole,
        scratch_shapes=[
            pltpu.VMEM((BS * BS, R), BF16),
            pltpu.VMEM((SLOTS, BS, BS * BS), jnp.int32),
            pltpu.SemaphoreType.DMA((SLOTS,)),
        ],
        out_shape=jax.ShapeDtypeStruct((RB1, BS, R), F32),
        compiler_params=pltpu.CompilerParams(vmem_limit_bytes=24 << 20),
        name="one_pass",
    )(coords, live, pltpu.with_memory_space_constraint(counts, pltpu.HBM), factor, both, rows_c)


def rounded(x):
    return lax.reduce_precision(x, exponent_bits=8, mantissa_bits=7)


def unweighted(factor, low):
    return jnp.where(low == 0.0, 0.0, factor / jnp.where(low == 0.0, 1.0, low))


def local(block_coords, live_blocks, counts, factor_a, factor_b, factor_c):
    coords = block_coords.reshape(SLOTS * 3)
    live = live_blocks.reshape(1)
    hits = counts.reshape(SLOTS, BS, BS * BS)
    low_a = rounded(factor_a)
    mine_b = lax.dynamic_slice_in_dim(factor_b, lax.axis_index(IA) * 4, 4, 0)
    column = from_everyone(jnp.concatenate([low_a.astype(F16), mine_b.astype(F16)], axis=0), ZK)
    share_b = lax.dynamic_slice_in_dim(column[:, 4:], lax.axis_index(JZ) * 8, 8, 0)
    both = from_everyone(
        jnp.concatenate([share_b.reshape(32, R), factor_c.T.astype(F16)], axis=0), IA
    ).astype(F32)
    low = from_everyone(column[:, :4].reshape(64, R).astype(BF16), JX).reshape(R, R)
    rows_c, mass = prepare(coords, live, both)

    phi = run_pass(coords, live, hits, low, both, rows_c)
    mass_rows = jnp.broadcast_to(
        (mass[:, 0, :] * MASS_SCALE).astype(F16).reshape(RB1, 1, 2, 128), (RB1, 16, 2, 128)
    ).reshape(64, 2, 128)
    sent = jnp.concatenate([phi.astype(F16).reshape(64, 2, 512), mass_rows], axis=2)
    got = swap(sent, JK).astype(F32).sum(axis=0)
    scale = (MASS_SCALE / PHI_SCALE) / got[:, 512:].reshape(1, R)
    first = unweighted(factor_a, low_a) * got[:, :512].reshape(4, R) * scale
    low_first = rounded(first)
    low = from_everyone(low_first.astype(BF16), JK).reshape(R, R)
    phi = run_pass(coords, live, hits, low, both, rows_c)
    mine = swap(phi.astype(F16).reshape(64, 4, R), JK).astype(F32).sum(axis=0)
    return unweighted(first, low_first) * mine * scale


def solution(mesh):
    shape = mesh.shape
    fine = Mesh(
        mesh.devices.reshape(shape["ia"], shape["ja"] // 2, 2, shape["ka"]), (IA, JX, JZ, KA)
    )
    placed = (
        P(IA, (JX, JZ), KA, None, None),
        P(IA, (JX, JZ), KA),
        P(IA, (JX, JZ), KA, None, None, None),
        P((IA, JX, JZ, KA), None),
        P((JX, JZ, KA), None),
        P(KA, IA),
    )
    return jax.shard_map(
        local, mesh=fine, in_specs=placed, out_specs=P((IA, JX, JZ, KA), None), check_vma=False
    )
```

time: 162 us -> 130 us (0.80)
  blocking collectives: 76.9 us -> 61.8 us
  waiting for transfers between devices: 30.8 us -> 21 us
  starting transfers between devices: 28.3 us -> 24.6 us
  local copies, waits for them, and re-layouts: 6.52 us -> 3.18 us
    all_to_all x5 -> x3, blocking collectives: 76.9 us -> 61.8 us  [swap(): return lax.all_to_all(x, axis, split_axis=0, concat_axis=0, tiled=True)]
    all_to_all x3, waiting for transfers between devices: 30.8 us -> 21 us  [swap(): return lax.all_to_all(x, axis, split_axis=0, concat_axis=0, tiled=True)]
    all_to_all x3, starting transfers between devices: 28.3 us -> 24.6 us  [swap(): return lax.all_to_all(x, axis, split_axis=0, concat_axis=0, tiled=True)]
  transfers between devices with their start and end apart: 3 -> 3, of which waited for: 3 -> 3; matrix products, arithmetic and copies ran while one was open for 2% -> 1% of each run, Pallas kernels for 0% -> 1%
where the time goes in v2:
time: 130 us; the launch traced here: 129 us
  blocking collectives  61.8 us (48%)
  starting transfers between devices  24.6 us (19%)
  waiting for transfers between devices  21 us (16%)
  Pallas kernels  15.3 us (12%)
  local copies, waits for them, and re-layouts  3.18 us (2%)
  other arithmetic  2.73 us (2%)
    all_to_all x3, blocking collectives, swap(): return lax.all_to_all(x, axis, split_axis=0, concat_axis=0, tiled=True)  61.8 us
    all_to_all x3, starting transfers between devices, swap(): return lax.all_to_all(x, axis, split_axis=0, concat_axis=0, tiled=True)  24.6 us
    all_to_all x3, waiting for transfers between devices, swap(): return lax.all_to_all(x, axis, split_axis=0, concat_axis=0, tiled=True)  21 us
    pallas_call x2, Pallas kernels, run_pass(): pl.pallas_call(pass_kernel, in_specs=[scalars, scalars, pl.BlockSpec(memo...  14.5 us
  transfers between devices with their start and end apart: 3, of which 3 were waited for; matrix products, arithmetic and copies ran while one was open for 1% of the time, Pallas kernels for 1%

profile of v2, /device:TPU:6, one launch (start us, length us, event | category | flops | bytes accessed | tf_op | source)
XLA Modules:
  0.0 129.4 jit_solution(10627386380687887629)
XLA Ops:
  0.0 0.7 reduce-precision_convert_fusion
  0.7 0.6 broadcast_in_dim.25
  1.4 15.2 %all-to-all-start = ((f16[16,8,256]{2,1,0:T(8,128)(2,1)}), f16[16,8,256]{2,1,0:T(8,128)(2,1)S(1)}, u32[]{:S(2)}, u32[]{:S(2)}) async-start(f16[16,8,256]{2,1,0:T(8,128)(2,1)} %broadcast_in_dim.25), calls=%async_computation | async-start | bytes 131072 | tf_op jit(solution)/shard_map/all_to_all | solution.py:29
  16.6 0.8 convert_bitcast_fusion
  17.3 12.0 %all-to-all-done = f16[16,8,256]{2,1,0:T(8,128)(2,1)S(1)} async-done(((f16[16,8,256]{2,1,0:T(8,128)(2,1)}), f16[16,8,256]{2,1,0:T(8,128)(2,1)S(1)}, u32[]{:S(2)}, u32[]{:S(2)}) %all-to-all-start) | async-done | bytes 65568 | tf_op jit(solution)/shard_map/all_to_all | solution.py:29
  29.4 0.7 broadcast_in_dim.27
  30.1 4.5 %all-to-all-start.2 = ((f16[8,64,256]{2,1,0:T(8,128)(2,1)}), f16[8,64,256]{2,1,0:T(8,128)(2,1)S(1)}, u32[]{:S(2)}, u32[]{:S(2)}) async-start(f16[8,64,256]{2,1,0:T(8,128)(2,1)} %broadcast_in_dim.27), calls=%async_computation.2 | async-start | bytes 524288 | tf_op jit(solution)/shard_map/all_to_all | solution.py:29
  35.2 0.8 copy.11
  36.0 0.1 reshape.52.coords
  36.1 6.0 %all-to-all-done.2 = f16[8,64,256]{2,1,0:T(8,128)(2,1)S(1)} async-done(((f16[8,64,256]{2,1,0:T(8,128)(2,1)}), f16[8,64,256]{2,1,0:T(8,128)(2,1)S(1)}, u32[]{:S(2)}, u32[]{:S(2)}) %all-to-all-start.2) | async-done | bytes 262176 | tf_op jit(solution)/shard_map/all_to_all | solution.py:29
  42.1 0.7 broadcast_in_dim.26
  42.7 0.0 copy-start
  42.7 4.9 %all-to-all-start.1 = ((bf16[4,64,256]{2,1,0:T(8,128)(2,1)}), bf16[4,64,256]{2,1,0:T(8,128)(2,1)S(1)}, u32[]{:S(2)}, u32[]{:S(2)}) async-start(bf16[4,64,256]{2,1,0:T(8,128)(2,1)} %broadcast_in_dim.26), calls=%async_computation.1 | async-start | bytes 262144 | tf_op jit(solution)/shard_map/all_to_all | solution.py:29
  47.7 0.8 prepare.1
  48.5 3.0 %all-to-all-done.1 = bf16[4,64,256]{2,1,0:T(8,128)(2,1)S(1)} async-done(((bf16[4,64,256]{2,1,0:T(8,128)(2,1)}), bf16[4,64,256]{2,1,0:T(8,128)(2,1)S(1)}, u32[]{:S(2)}, u32[]{:S(2)}) %all-to-all-start.1) | async-done | bytes 131104 | tf_op jit(solution)/shard_map/all_to_all | solution.py:29
  51.6 7.2 %one_pass.2 = f32[4,64,256]{2,1,0:T(8,128)S(1)} custom-call(s32[12]{0:T(128)S(1)} %reshape.52.coords, s32[1]{0:T(128)} %bitcast.12.live, s32[4,64,4096]{2,1,0:T(8,128)} %bitcast.15, bf16[256,256]{1,0:T(8,128)(2,1)S(1)} %bitcast.14, f32[8,64,256]{2,1,0:T(8,128)S(1)} %convert_element_type.52.both, f32[256,256]{1,0:T(8,128)S(1)} %get-tuple-element.7.rows_c), custom_call_target="tpu_custom_call" | custom-call | tf_op jit(solution)/shard_map/one_pass/pallas_call | solution.py:123
  58.8 0.1 reshape.57
  59.0 0.2 pad_maximum_fusion
  59.2 21.1 %all_to_all.30 = f16[64,2,640]{2,1,0:T(2,128)(2,1)S(1)} all-to-all(f16[64,2,640]{2,1,0:T(2,128)(2,1)S(1)} %pad_maximum_fusion), channel_id=1, replica_groups=mesh['ia'=8,'jx'=4,'jz'=2,'ka'=8] {'jx','jz','ka'}, dimensions={0} | all-to-all | bytes 327680 | tf_op jit(solution)/shard_map/all_to_all | solution.py:29
  80.3 0.2 convert_reduce_fusion
  80.5 0.0 copy-done
  80.5 20.5 %all_to_all.31 = bf16[64,4,256]{2,1,0:T(4,128)(2,1)S(1)} all-to-all(bf16[64,4,256]{2,1,0:T(4,128)(2,1)S(1)} %broadcast_in_dim.29), channel_id=1, replica_groups=mesh['ia'=8,'jx'=4,'jz'=2,'ka'=8] {'jx','jz','ka'}, dimensions={0} | all-to-all | bytes 262144 | tf_op jit(solution)/shard_map/all_to_all | solution.py:29
  101.1 7.2 %one_pass.3 = f32[4,64,256]{2,1,0:T(8,128)S(1)} custom-call(s32[12]{0:T(128)S(1)} %reshape.52.coords, s32[1]{0:T(128)} %bitcast.13.live, s32[4,64,4096]{2,1,0:T(8,128)} %bitcast.16, bf16[256,256]{1,0:T(8,128)(2,1)S(1)} %reshape.60.factor, f32[8,64,256]{2,1,0:T(8,128)S(1)} %convert_element_type.52.both, f32[256,256]{1,0:T(8,128)S(1)} %get-tuple-element.7.rows_c), custom_call_target="tpu_custom_call" | custom-call | tf_op jit(solution)/shard_map/one_pass/pallas_call | solution.py:123
  108.4 20.2 %all_to_all.32 = f16[64,4,256]{2,1,0:T(4,128)(2,1)S(1)} all-to-all(f16[64,4,256]{2,1,0:T(4,128)(2,1)S(1)} %reshape.61), channel_id=1, replica_groups=mesh['ia'=8,'jx'=4,'jz'=2,'ka'=8] {'jx','jz','ka'}, dimensions={0} | all-to-all | bytes 262144 | tf_op jit(solution)/shard_map/all_to_all | solution.py:29
  128.7 0.1 convert_reduce_fusion.1
  128.7 0.6 fusion.4
  (20 shorter events, 0.4 us)
Async XLA Ops:
  1.4 27.9 %all-to-all-start = ((f16[16,8,256]{2,1,0:T(8,128)(2,1)}), f16[16,8,256]{2,1,0:T(8,128)(2,1)S(1)}, u32[]{:S(2)}, u32[]{:S(2)}) async-start(f16[16,8,256]{2,1,0:T(8,128)(2,1)} %broadcast_in_dim.25), calls=%async_computation | async-start | bytes 131072 | tf_op jit(solution)/shard_map/all_to_all | solution.py:29
  30.1 12.0 %all-to-all-start.2 = ((f16[8,64,256]{2,1,0:T(8,128)(2,1)}), f16[8,64,256]{2,1,0:T(8,128)(2,1)S(1)}, u32[]{:S(2)}, u32[]{:S(2)}) async-start(f16[8,64,256]{2,1,0:T(8,128)(2,1)} %broadcast_in_dim.27), calls=%async_computation.2 | async-start | bytes 524288 | tf_op jit(solution)/shard_map/all_to_all | solution.py:29
  42.7 37.7 %copy-start = (f32[4,256]{1,0:T(4,128)S(1)}, f32[4,256]{1,0:T(4,128)}, u32[]{:S(2)}) copy-start(f32[4,256]{1,0:T(4,128)} %param.9) | copy-start | bytes 12292
  42.7 8.8 %all-to-all-start.1 = ((bf16[4,64,256]{2,1,0:T(8,128)(2,1)}), bf16[4,64,256]{2,1,0:T(8,128)(2,1)S(1)}, u32[]{:S(2)}, u32[]{:S(2)}) async-start(bf16[4,64,256]{2,1,0:T(8,128)(2,1)} %broadcast_in_dim.26), calls=%async_computation.1 | async-start | bytes 262144 | tf_op jit(solution)/shard_map/all_to_all | solution.py:29

commit v3 on v2

--- a/solution.py
+++ b/solution.py
@@ -37,6 +37,47 @@
     return pl.ds(pl.multiple_of(start * size, size), size)
 
 
+def whole():
+    return pl.BlockSpec(memory_space=pltpu.VMEM)
+
+
+def scalars():
+    return pl.BlockSpec(memory_space=pltpu.SMEM)
+
+
+def load_kernel(live, counts, hits, raw, arrived):
+    def fetch(slot):
+        return pltpu.make_async_copy(counts.at[slot], raw.at[slot], arrived.at[slot])
+
+    for slot in range(SLOTS):
+
+        @pl.when(slot < live[0])
+        def _():
+            fetch(slot).start()
+
+    def step(slot, carry):
+        fetch(slot).wait()
+        hits[slot] = raw[slot].astype(F32).astype(BF16)
+        return carry
+
+    lax.fori_loop(0, live[0], step, 0)
+
+
+def load(live, counts):
+    return pl.pallas_call(
+        load_kernel,
+        in_specs=[scalars(), pl.BlockSpec(memory_space=pltpu.HBM)],
+        out_specs=whole(),
+        out_shape=jax.ShapeDtypeStruct((SLOTS, BS, BS * BS), BF16),
+        scratch_shapes=[
+            pltpu.VMEM((SLOTS, BS, BS * BS), jnp.int32),
+            pltpu.SemaphoreType.DMA((SLOTS,)),
+        ],
+        compiler_params=pltpu.CompilerParams(vmem_limit_bytes=10 << 20),
+        name="load",
+    )(live, pltpu.with_memory_space_constraint(counts, pltpu.HBM))
+
+
 def block_order(eighth, half):
     return half * 8 + eighth
 
@@ -59,12 +100,10 @@
 
 
 def prepare(coords, live, both):
-    whole = pl.BlockSpec(memory_space=pltpu.VMEM)
-    scalars = pl.BlockSpec(memory_space=pltpu.SMEM)
     return pl.pallas_call(
         prep_kernel,
-        in_specs=[scalars, scalars, whole],
-        out_specs=[whole, whole],
+        in_specs=[scalars(), scalars(), whole()],
+        out_specs=[whole(), whole()],
         out_shape=[
             jax.ShapeDtypeStruct((R, R), F32),
             jax.ShapeDtypeStruct((RB1, 8, R), F32),
@@ -74,16 +113,7 @@
     )(coords, live, both)
 
 
-def pass_kernel(coords, live, counts, factor, both, rows_c, out, panel, hits, arrived):
-    def fetch(slot):
-        return pltpu.make_async_copy(counts.at[slot], hits.at[slot], arrived.at[slot])
-
-    for slot in range(SLOTS):
-
-        @pl.when(slot < live[0])
-        def _():
-            fetch(slot).start()
-
+def pass_kernel(coords, live, hits, factor, both, rows_c, out, panel):
     out[...] = jnp.zeros_like(out)
 
     def step(slot, carry):
@@ -101,7 +131,6 @@
                     panel[(first + q) * BS : (first + q + 1) * BS, :] = (
                         row * piece_c
                     ).astype(BF16)
-        fetch(slot).wait()
         total = jnp.zeros((BS, R), F32)
         for start in range(0, BS * BS, SPAN):
             piece = panel[start : start + SPAN, :]
@@ -117,22 +146,16 @@
     lax.fori_loop(0, live[0], step, 0)
 
 
-def run_pass(coords, live, counts, factor, both, rows_c):
-    whole = pl.BlockSpec(memory_space=pltpu.VMEM)
-    scalars = pl.BlockSpec(memory_space=pltpu.SMEM)
+def run_pass(coords, live, hits, factor, both, rows_c):
     return pl.pallas_call(
         pass_kernel,
-        in_specs=[scalars, scalars, pl.BlockSpec(memory_space=pltpu.HBM), whole, whole, whole],
-        out_specs=whole,
-        scratch_shapes=[
-            pltpu.VMEM((BS * BS, R), BF16),
-            pltpu.VMEM((SLOTS, BS, BS * BS), jnp.int32),
-            pltpu.SemaphoreType.DMA((SLOTS,)),
-        ],
+        in_specs=[scalars(), scalars()] + [whole()] * 4,
+        out_specs=whole(),
+        scratch_shapes=[pltpu.VMEM((BS * BS, R), BF16)],
         out_shape=jax.ShapeDtypeStruct((RB1, BS, R), F32),
-        compiler_params=pltpu.CompilerParams(vmem_limit_bytes=24 << 20),
+        compiler_params=pltpu.CompilerParams(vmem_limit_bytes=16 << 20),
         name="one_pass",
-    )(coords, live, pltpu.with_memory_space_constraint(counts, pltpu.HBM), factor, both, rows_c)
+    )(coords, live, hits, factor, both, rows_c)
 
 
 def rounded(x):
@@ -146,10 +169,10 @@
 def local(block_coords, live_blocks, counts, factor_a, factor_b, factor_c):
     coords = block_coords.reshape(SLOTS * 3)
     live = live_blocks.reshape(1)
-    hits = counts.reshape(SLOTS, BS, BS * BS)
     low_a = rounded(factor_a)
     mine_b = lax.dynamic_slice_in_dim(factor_b, lax.axis_index(IA) * 4, 4, 0)
     column = from_everyone(jnp.concatenate([low_a.astype(F16), mine_b.astype(F16)], axis=0), ZK)
+    hits = load(live, counts.reshape(SLOTS, BS, BS * BS))
     share_b = lax.dynamic_slice_in_dim(column[:, 4:], lax.axis_index(JZ) * 8, 8, 0)
     both = from_everyone(
         jnp.concatenate([share_b.reshape(32, R), factor_c.T.astype(F16)], axis=0), IA

time: 130 us -> 126 us (0.969)
  waiting for transfers between devices: 21 us -> 18.7 us
  Pallas kernels: 15.3 us -> 13.5 us
    all_to_all x3, waiting for transfers between devices: 21 us -> 18.7 us  [swap(): return lax.all_to_all(x, axis, split_axis=0, concat_axis=0, tiled=True)]
    pallas_call x3 -> x4, Pallas kernels: 15.3 us -> 13.5 us  [the longest x2 10.5 us: run_pass(): pl.pallas_call(pass_kernel, in_specs=[scalars(), scalars()] + [whole()] *...]
  transfers between devices with their start and end apart: 3 -> 3, of which waited for: 3 -> 3; matrix products, arithmetic and copies ran while one was open for 1% -> 1% of each run, Pallas kernels for 1% -> 2%
where the time goes in v3:
time: 126 us; the launch traced here: 125 us
  blocking collectives  61.8 us (49%)
  starting transfers between devices  24.4 us (19%)
  waiting for transfers between devices  18.7 us (15%)
  Pallas kernels  13.5 us (11%)
  local copies, waits for them, and re-layouts  3.18 us (3%)
  other arithmetic  2.73 us (2%)
    all_to_all x3, blocking collectives, swap(): return lax.all_to_all(x, axis, split_axis=0, concat_axis=0, tiled=True)  61.8 us
    all_to_all x3, starting transfers between devices, swap(): return lax.all_to_all(x, axis, split_axis=0, concat_axis=0, tiled=True)  24.4 us
    all_to_all x3, waiting for transfers between devices, swap(): return lax.all_to_all(x, axis, split_axis=0, concat_axis=0, tiled=True)  18.7 us
    pallas_call x2, Pallas kernels, run_pass(): pl.pallas_call(pass_kernel, in_specs=[scalars(), scalars()] + [whole()] *...  10.5 us
  transfers between devices with their start and end apart: 3, of which 3 were waited for; matrix products, arithmetic and copies ran while one was open for 1% of the time, Pallas kernels for 2%

profile of v3, /device:TPU:6, one launch (start us, length us, event | category | flops | bytes accessed | tf_op | source)
XLA Modules:
  0.0 125.2 jit_solution(8438353065911233444)
XLA Ops:
  0.0 0.7 reduce-precision_convert_fusion
  0.7 0.6 broadcast_in_dim.25
  1.4 15.2 %all-to-all-start = ((f16[16,8,256]{2,1,0:T(8,128)(2,1)}), f16[16,8,256]{2,1,0:T(8,128)(2,1)S(1)}, u32[]{:S(2)}, u32[]{:S(2)}) async-start(f16[16,8,256]{2,1,0:T(8,128)(2,1)} %broadcast_in_dim.25), calls=%async_computation | async-start | bytes 131072 | tf_op jit(solution)/shard_map/all_to_all | solution.py:29
  16.6 0.8 convert_bitcast_fusion
  17.3 12.0 %all-to-all-done = f16[16,8,256]{2,1,0:T(8,128)(2,1)S(1)} async-done(((f16[16,8,256]{2,1,0:T(8,128)(2,1)}), f16[16,8,256]{2,1,0:T(8,128)(2,1)S(1)}, u32[]{:S(2)}, u32[]{:S(2)}) %all-to-all-start) | async-done | bytes 65568 | tf_op jit(solution)/shard_map/all_to_all | solution.py:29
  29.4 0.7 broadcast_in_dim.27
  30.1 4.5 %all-to-all-start.2 = ((f16[8,64,256]{2,1,0:T(8,128)(2,1)}), f16[8,64,256]{2,1,0:T(8,128)(2,1)S(1)}, u32[]{:S(2)}, u32[]{:S(2)}) async-start(f16[8,64,256]{2,1,0:T(8,128)(2,1)} %broadcast_in_dim.27), calls=%async_computation.2 | async-start | bytes 524288 | tf_op jit(solution)/shard_map/all_to_all | solution.py:29
  35.2 0.8 copy.11
  36.0 0.1 reshape.52.coords
  36.1 2.3 %load.1.hits = bf16[4,64,4096]{2,1,0:T(8,128)(2,1)S(1)} custom-call(s32[1]{0:T(128)} %bitcast.11.live, s32[4,64,4096]{2,1,0:T(8,128)} %bitcast.16), custom_call_target="tpu_custom_call" | custom-call | tf_op jit(solution)/shard_map/load/pallas_call | solution.py:67
  38.4 0.0 copy-start
  38.4 3.7 %all-to-all-done.2 = f16[8,64,256]{2,1,0:T(8,128)(2,1)S(1)} async-done(((f16[8,64,256]{2,1,0:T(8,128)(2,1)}), f16[8,64,256]{2,1,0:T(8,128)(2,1)S(1)}, u32[]{:S(2)}, u32[]{:S(2)}) %all-to-all-start.2) | async-done | bytes 262176 | tf_op jit(solution)/shard_map/all_to_all | solution.py:29
  42.1 0.7 broadcast_in_dim.26
  42.7 4.8 %all-to-all-start.1 = ((bf16[4,64,256]{2,1,0:T(8,128)(2,1)}), bf16[4,64,256]{2,1,0:T(8,128)(2,1)S(1)}, u32[]{:S(2)}, u32[]{:S(2)}) async-start(bf16[4,64,256]{2,1,0:T(8,128)(2,1)} %broadcast_in_dim.26), calls=%async_computation.1 | async-start | bytes 262144 | tf_op jit(solution)/shard_map/all_to_all | solution.py:29
  47.6 0.8 prepare.1
  48.4 3.0 %all-to-all-done.1 = bf16[4,64,256]{2,1,0:T(8,128)(2,1)S(1)} async-done(((bf16[4,64,256]{2,1,0:T(8,128)(2,1)}), bf16[4,64,256]{2,1,0:T(8,128)(2,1)S(1)}, u32[]{:S(2)}, u32[]{:S(2)}) %all-to-all-start.1) | async-done | bytes 131104 | tf_op jit(solution)/shard_map/all_to_all | solution.py:29
  51.4 5.2 %one_pass.2 = f32[4,64,256]{2,1,0:T(8,128)S(1)} custom-call(s32[12]{0:T(128)S(1)} %reshape.52.coords, s32[1]{0:T(128)} %bitcast.13.live, bf16[4,64,4096]{2,1,0:T(8,128)(2,1)S(1)} %load.1.hits, bf16[256,256]{1,0:T(8,128)(2,1)S(1)} %bitcast.15, f32[8,64,256]{2,1,0:T(8,128)S(1)} %convert_element_type.52.both, f32[256,256]{1,0:T(8,128)S(1)} %get-tuple-element.7.rows_c), custom_call_target="tpu_custom_call" | custom-call | tf_op jit(solution)/shard_map/one_pass/pallas_call | solution.py:150
  56.7 0.1 reshape.57
  56.8 0.2 pad_maximum_fusion
  57.1 21.1 %all_to_all.30 = f16[64,2,640]{2,1,0:T(2,128)(2,1)S(1)} all-to-all(f16[64,2,640]{2,1,0:T(2,128)(2,1)S(1)} %pad_maximum_fusion), channel_id=1, replica_groups=mesh['ia'=8,'jx'=4,'jz'=2,'ka'=8] {'jx','jz','ka'}, dimensions={0} | all-to-all | bytes 327680 | tf_op jit(solution)/shard_map/all_to_all | solution.py:29
  78.1 0.2 convert_reduce_fusion
  78.3 0.0 copy-done
  78.4 20.5 %all_to_all.31 = bf16[64,4,256]{2,1,0:T(4,128)(2,1)S(1)} all-to-all(bf16[64,4,256]{2,1,0:T(4,128)(2,1)S(1)} %broadcast_in_dim.29), channel_id=1, replica_groups=mesh['ia'=8,'jx'=4,'jz'=2,'ka'=8] {'jx','jz','ka'}, dimensions={0} | all-to-all | bytes 262144 | tf_op jit(solution)/shard_map/all_to_all | solution.py:29
  99.0 5.2 %one_pass.3 = f32[4,64,256]{2,1,0:T(8,128)S(1)} custom-call(s32[12]{0:T(128)S(1)} %reshape.52.coords, s32[1]{0:T(128)} %bitcast.14.live, bf16[4,64,4096]{2,1,0:T(8,128)(2,1)S(1)} %load.1.hits, bf16[256,256]{1,0:T(8,128)(2,1)S(1)} %reshape.60.factor, f32[8,64,256]{2,1,0:T(8,128)S(1)} %convert_element_type.52.both, f32[256,256]{1,0:T(8,128)S(1)} %get-tuple-element.7.rows_c), custom_call_target="tpu_custom_call" | custom-call | tf_op jit(solution)/shard_map/one_pass/pallas_call | solution.py:150
  104.3 20.2 %all_to_all.32 = f16[64,4,256]{2,1,0:T(4,128)(2,1)S(1)} all-to-all(f16[64,4,256]{2,1,0:T(4,128)(2,1)S(1)} %reshape.61), channel_id=1, replica_groups=mesh['ia'=8,'jx'=4,'jz'=2,'ka'=8] {'jx','jz','ka'}, dimensions={0} | all-to-all | bytes 262144 | tf_op jit(solution)/shard_map/all_to_all | solution.py:29
  124.5 0.1 convert_reduce_fusion.1
  124.6 0.6 fusion.4
  (20 shorter events, 0.4 us)
Async XLA Ops:
  1.4 27.9 %all-to-all-start = ((f16[16,8,256]{2,1,0:T(8,128)(2,1)}), f16[16,8,256]{2,1,0:T(8,128)(2,1)S(1)}, u32[]{:S(2)}, u32[]{:S(2)}) async-start(f16[16,8,256]{2,1,0:T(8,128)(2,1)} %broadcast_in_dim.25), calls=%async_computation | async-start | bytes 131072 | tf_op jit(solution)/shard_map/all_to_all | solution.py:29
  30.1 12.0 %all-to-all-start.2 = ((f16[8,64,256]{2,1,0:T(8,128)(2,1)}), f16[8,64,256]{2,1,0:T(8,128)(2,1)S(1)}, u32[]{:S(2)}, u32[]{:S(2)}) async-start(f16[8,64,256]{2,1,0:T(8,128)(2,1)} %broadcast_in_dim.27), calls=%async_computation.2 | async-start | bytes 524288 | tf_op jit(solution)/shard_map/all_to_all | solution.py:29
  38.4 40.0 %copy-start = (f32[4,256]{1,0:T(4,128)S(1)}, f32[4,256]{1,0:T(4,128)}, u32[]{:S(2)}) copy-start(f32[4,256]{1,0:T(4,128)} %param.9) | copy-start | bytes 12292
  42.7 8.7 %all-to-all-start.1 = ((bf16[4,64,256]{2,1,0:T(8,128)(2,1)}), bf16[4,64,256]{2,1,0:T(8,128)(2,1)S(1)}, u32[]{:S(2)}, u32[]{:S(2)}) async-start(bf16[4,64,256]{2,1,0:T(8,128)(2,1)} %broadcast_in_dim.26), calls=%async_computation.1 | async-start | bytes 262144 | tf_op jit(solution)/shard_map/all_to_all | solution.py:29

commit v4 on v3

--- a/solution.py
+++ b/solution.py
@@ -1,3 +1,5 @@
+import functools
+
 import jax
 import jax.numpy as jnp
 from jax import lax
@@ -16,6 +18,7 @@
 PHI_SCALE = 0.25
 MASS_SCALE = 1.0 / 32.0
 BF16 = jnp.bfloat16
+
 
 IA = "ia"
 JX = "jx"
@@ -113,14 +116,20 @@
     )(coords, live, both)
 
 
-def pass_kernel(coords, live, hits, factor, both, rows_c, out, panel):
+def pass_kernel(pieces, coords, live, hits, both, rows_c, *rest):
+    if pieces:
+        place, *parts, out, panel, factor = rest
+        for back in range(RB1):
+            factor[back * BS : (back + 1) * BS, :] = parts[back][...]
+    else:
+        factor, out, panel = rest
     out[...] = jnp.zeros_like(out)
 
     def step(slot, carry):
         i = coords[slot * 3]
         j = coords[slot * 3 + 1]
         k = coords[slot * 3 + 2]
-        piece_a = factor[aligned(i, BS), :]
+        piece_a = factor[aligned((place[0] - i) & (RB1 - 1) if pieces else i, BS), :]
         piece_c = rows_c[aligned(k, BS), :]
         for half in range(2):
             for eighth in range(8):
@@ -146,16 +155,22 @@
     lax.fori_loop(0, live[0], step, 0)
 
 
-def run_pass(coords, live, hits, factor, both, rows_c):
+def run_pass(coords, live, hits, both, rows_c, place, *factor):
+    pieces = place is not None
+    scratch = [pltpu.VMEM((BS * BS, R), BF16)]
+    if pieces:
+        scratch.append(pltpu.VMEM((R, R), BF16))
     return pl.pallas_call(
-        pass_kernel,
-        in_specs=[scalars(), scalars()] + [whole()] * 4,
+        functools.partial(pass_kernel, pieces),
+        in_specs=[scalars(), scalars(), whole(), whole(), whole()]
+        + ([scalars()] if pieces else [])
+        + [whole()] * len(factor),
         out_specs=whole(),
-        scratch_shapes=[pltpu.VMEM((BS * BS, R), BF16)],
+        scratch_shapes=scratch,
         out_shape=jax.ShapeDtypeStruct((RB1, BS, R), F32),
         compiler_params=pltpu.CompilerParams(vmem_limit_bytes=16 << 20),
         name="one_pass",
-    )(coords, live, hits, factor, both, rows_c)
+    )(coords, live, hits, both, rows_c, *([place] if pieces else []), *factor)
 
 
 def rounded(x):
@@ -177,10 +192,16 @@
     both = from_everyone(
         jnp.concatenate([share_b.reshape(32, R), factor_c.T.astype(F16)], axis=0), IA
     ).astype(F32)
-    low = from_everyone(column[:, :4].reshape(64, R).astype(BF16), JX).reshape(R, R)
+    own = column[:, :4].reshape(BS, R).astype(BF16)
+    many = lax.axis_size(JX)
+    pieces = [own] + [
+        lax.ppermute(own, JX, [(x, (x + back) % many) for x in range(many)])
+        for back in range(1, many)
+    ]
     rows_c, mass = prepare(coords, live, both)
 
-    phi = run_pass(coords, live, hits, low, both, rows_c)
+    place = lax.axis_index(JX).reshape(1)
+    phi = run_pass(coords, live, hits, both, rows_c, place, *pieces)
     mass_rows = jnp.broadcast_to(
         (mass[:, 0, :] * MASS_SCALE).astype(F16).reshape(RB1, 1, 2, 128), (RB1, 16, 2, 128)
     ).reshape(64, 2, 128)
@@ -190,7 +211,7 @@
     first = unweighted(factor_a, low_a) * got[:, :512].reshape(4, R) * scale
     low_first = rounded(first)
     low = from_everyone(low_first.astype(BF16), JK).reshape(R, R)
-    phi = run_pass(coords, live, hits, low, both, rows_c)
+    phi = run_pass(coords, live, hits, both, rows_c, None, low)
     mine = swap(phi.astype(F16).reshape(64, 4, R), JK).astype(F32).sum(axis=0)
     return unweighted(first, low_first) * mine * scale
 

time: 126 us -> 127 us (level)
  waiting for transfers between devices: 18.7 us -> 13.6 us
  starting transfers between devices: 24.4 us -> 28.8 us
  blocking collectives: 61.8 us -> 63.3 us
    ppermute x0 -> x3, starting transfers between devices: none -> 9.13 us  [local(): lax.ppermute(own, JX, [(x, (x + back) % many) for x in range(many)])]
    all_to_all x3 -> x2, waiting for transfers between devices: 18.7 us -> 12 us  [swap(): return lax.all_to_all(x, axis, split_axis=0, concat_axis=0, tiled=True)]
    all_to_all x3 -> x2, starting transfers between devices: 24.4 us -> 19.7 us  [swap(): return lax.all_to_all(x, axis, split_axis=0, concat_axis=0, tiled=True)]
    ppermute x0 -> x3, waiting for transfers between devices: none -> 1.66 us  [local(): lax.ppermute(own, JX, [(x, (x + back) % many) for x in range(many)])]
    all_to_all x3, blocking collectives: 61.8 us -> 63.3 us  [swap(): return lax.all_to_all(x, axis, split_axis=0, concat_axis=0, tiled=True)]
  transfers between devices with their start and end apart: 3 -> 5, of which waited for: 3 -> 2; matrix products, arithmetic and copies ran while one was open for 1% -> 1% of each run, Pallas kernels for 2% -> 2%
where the time goes in v4:
time: 127 us; the launch traced here: 125 us
  blocking collectives  63.3 us (50%)
  starting transfers between devices  28.8 us (23%)
  waiting for transfers between devices  13.6 us (11%)
  Pallas kernels  13.5 us (11%)
  other arithmetic  2.73 us (2%)
  local copies, waits for them, and re-layouts  2.55 us (2%)
    all_to_all x3, blocking collectives, swap(): return lax.all_to_all(x, axis, split_axis=0, concat_axis=0, tiled=True)  63.3 us
    all_to_all x2, starting transfers between devices, swap(): return lax.all_to_all(x, axis, split_axis=0, concat_axis=0, tiled=True)  19.7 us
    all_to_all x2, waiting for transfers between devices, swap(): return lax.all_to_all(x, axis, split_axis=0, concat_axis=0, tiled=True)  12 us
    pallas_call x2, Pallas kernels, run_pass(): pl.pallas_call(functools.partial(pass_kernel, pieces), in_specs=[scalars(...  10.5 us
    ppermute x3, starting transfers between devices, local(): lax.ppermute(own, JX, [(x, (x + back) % many) for x in range(many)])  9.13 us
  transfers between devices with their start and end apart: 5, of which 2 were waited for; matrix products, arithmetic and copies ran while one was open for 1% of the time, Pallas kernels for 2%

profile of v4, /device:TPU:6, one launch (start us, length us, event | category | flops | bytes accessed | tf_op | source)
XLA Modules:
  0.0 125.4 jit_solution(746481324612649087)
XLA Ops:
  0.0 0.7 reduce-precision_convert_fusion
  0.7 0.6 broadcast_in_dim.22
  1.4 15.2 %all-to-all-start = ((f16[16,8,256]{2,1,0:T(8,128)(2,1)}), f16[16,8,256]{2,1,0:T(8,128)(2,1)S(1)}, u32[]{:S(2)}, u32[]{:S(2)}) async-start(f16[16,8,256]{2,1,0:T(8,128)(2,1)} %broadcast_in_dim.22), calls=%async_computation | async-start | bytes 131072 | tf_op jit(solution)/shard_map/all_to_all | solution.py:32
  16.6 0.8 convert_bitcast_fusion
  17.3 12.0 %all-to-all-done = f16[16,8,256]{2,1,0:T(8,128)(2,1)S(1)} async-done(((f16[16,8,256]{2,1,0:T(8,128)(2,1)}), f16[16,8,256]{2,1,0:T(8,128)(2,1)S(1)}, u32[]{:S(2)}, u32[]{:S(2)}) %all-to-all-start) | async-done | bytes 65568 | tf_op jit(solution)/shard_map/all_to_all | solution.py:32
  29.4 0.7 broadcast_in_dim.23
  30.1 4.5 %all-to-all-start.1 = ((f16[8,64,256]{2,1,0:T(8,128)(2,1)}), f16[8,64,256]{2,1,0:T(8,128)(2,1)S(1)}, u32[]{:S(2)}, u32[]{:S(2)}) async-start(f16[8,64,256]{2,1,0:T(8,128)(2,1)} %broadcast_in_dim.23), calls=%async_computation.1 | async-start | bytes 524288 | tf_op jit(solution)/shard_map/all_to_all | solution.py:32
  35.2 0.8 copy.11
  36.0 0.1 reshape.52.coords
  36.1 2.3 %load.1.hits = bf16[4,64,4096]{2,1,0:T(8,128)(2,1)S(1)} custom-call(s32[1]{0:T(128)} %bitcast.11.live, s32[4,64,4096]{2,1,0:T(8,128)} %bitcast.15), custom_call_target="tpu_custom_call" | custom-call | tf_op jit(solution)/shard_map/load/pallas_call | solution.py:70
  38.4 0.0 copy-start
  38.4 2.1 %collective-permute-start.2 = (bf16[64,256]{1,0:T(8,128)(2,1)S(1)}, bf16[64,256]{1,0:T(8,128)(2,1)S(1)}, u32[]{:S(2)}, u32[]{:S(2)}) collective-permute-start(bf16[64,256]{1,0:T(8,128)(2,1)S(1)} %convert_element_type.51.rest_1_), channel_id=1, source_target_pairs={{0,48},{16,0},{32,16},{48,32},{1,49},{17,1},{33,17},{49,33},{2,50}... | collective-permute-start | bytes 98312 | tf_op jit(solution)/shard_map/ppermute | solution.py:198
  40.5 2.7 %collective-permute-start.1 = (bf16[64,256]{1,0:T(8,128)(2,1)S(1)}, bf16[64,256]{1,0:T(8,128)(2,1)S(1)}, u32[]{:S(2)}, u32[]{:S(2)}) collective-permute-start(bf16[64,256]{1,0:T(8,128)(2,1)S(1)} %convert_element_type.51.rest_1_), channel_id=1, source_target_pairs={{0,32},{16,48},{32,0},{48,16},{1,33},{17,49},{33,1},{49,17},{2,34}... | collective-permute-start | bytes 98312 | tf_op jit(solution)/shard_map/ppermute | solution.py:198
  43.2 4.3 %collective-permute-start = (bf16[64,256]{1,0:T(8,128)(2,1)S(1)}, bf16[64,256]{1,0:T(8,128)(2,1)S(1)}, u32[]{:S(2)}, u32[]{:S(2)}) collective-permute-start(bf16[64,256]{1,0:T(8,128)(2,1)S(1)} %convert_element_type.51.rest_1_), channel_id=1, source_target_pairs={{0,16},{16,32},{32,48},{48,0},{1,17},{17,33},{33,49},{49,1},{2,18}... | collective-permute-start | bytes 98312 | tf_op jit(solution)/shard_map/ppermute | solution.py:198
  47.6 0.0 all-to-all-done.1
  47.6 0.8 prepare.1
  48.5 0.0 collective-permute-done.2.rest_4_
  48.5 0.0 collective-permute-done.1.rest_3_
  48.5 1.7 %collective-permute-done.rest_2_ = bf16[64,256]{1,0:T(8,128)(2,1)S(1)} collective-permute-done((bf16[64,256]{1,0:T(8,128)(2,1)S(1)}, bf16[64,256]{1,0:T(8,128)(2,1)S(1)}, u32[]{:S(2)}, u32[]{:S(2)}) %collective-permute-start) | collective-permute-done | bytes 32800 | tf_op jit(solution)/shard_map/ppermute | solution.py:198
  50.1 5.2 %one_pass.2 = f32[4,64,256]{2,1,0:T(8,128)S(1)} custom-call(s32[12]{0:T(128)S(1)} %reshape.52.coords, s32[1]{0:T(128)} %bitcast.13.live, bf16[4,64,4096]{2,1,0:T(8,128)(2,1)S(1)} %load.1.hits, f32[8,64,256]{2,1,0:T(8,128)S(1)} %convert_element_type.49.both, f32[256,256]{1,0:T(8,128)S(1)} %get-tuple-element.7.rows_c, s32[1]{0:T(128)} %bitcast.3.rest_0_, ...), custom_call_target="tpu_custom_call" | custom-call | tf_op jit(solution)/shard_map/one_pass/pallas_call | solution.py:163
  55.4 0.1 reshape.57
  55.5 0.2 pad_maximum_fusion
  55.8 22.6 %all_to_all.25 = f16[64,2,640]{2,1,0:T(2,128)(2,1)S(1)} all-to-all(f16[64,2,640]{2,1,0:T(2,128)(2,1)S(1)} %pad_maximum_fusion), channel_id=1, replica_groups=mesh['ia'=8,'jx'=4,'jz'=2,'ka'=8] {'jx','jz','ka'}, dimensions={0} | all-to-all | bytes 327680 | tf_op jit(solution)/shard_map/all_to_all | solution.py:32
  78.4 0.2 convert_reduce_fusion
  78.5 0.0 copy-done
  78.6 20.6 %all_to_all.26 = bf16[64,4,256]{2,1,0:T(4,128)(2,1)S(1)} all-to-all(bf16[64,4,256]{2,1,0:T(4,128)(2,1)S(1)} %broadcast_in_dim.25), channel_id=1, replica_groups=mesh['ia'=8,'jx'=4,'jz'=2,'ka'=8] {'jx','jz','ka'}, dimensions={0} | all-to-all | bytes 262144 | tf_op jit(solution)/shard_map/all_to_all | solution.py:32
  99.3 5.2 %one_pass.3 = f32[4,64,256]{2,1,0:T(8,128)S(1)} custom-call(s32[12]{0:T(128)S(1)} %reshape.52.coords, s32[1]{0:T(128)} %bitcast.14.live, bf16[4,64,4096]{2,1,0:T(8,128)(2,1)S(1)} %load.1.hits, f32[8,64,256]{2,1,0:T(8,128)S(1)} %convert_element_type.49.both, f32[256,256]{1,0:T(8,128)S(1)} %get-tuple-element.7.rows_c, bf16[256,256]{1,0:T(8,128)(2,1)S(1)} %reshape.60.rest_0_), custom_call_target="tpu_custom_call" | custom-call | tf_op jit(solution)/shard_map/one_pass/pallas_call | solution.py:163
  104.6 20.1 %all_to_all.27 = f16[64,4,256]{2,1,0:T(4,128)(2,1)S(1)} all-to-all(f16[64,4,256]{2,1,0:T(4,128)(2,1)S(1)} %reshape.61), channel_id=1, replica_groups=mesh['ia'=8,'jx'=4,'jz'=2,'ka'=8] {'jx','jz','ka'}, dimensions={0} | all-to-all | bytes 262144 | tf_op jit(solution)/shard_map/all_to_all | solution.py:32
  124.7 0.1 convert_reduce_fusion.1
  124.8 0.6 fusion.4
  (20 shorter events, 0.4 us)
Async XLA Ops:
  1.4 27.9 %all-to-all-start = ((f16[16,8,256]{2,1,0:T(8,128)(2,1)}), f16[16,8,256]{2,1,0:T(8,128)(2,1)S(1)}, u32[]{:S(2)}, u32[]{:S(2)}) async-start(f16[16,8,256]{2,1,0:T(8,128)(2,1)} %broadcast_in_dim.22), calls=%async_computation | async-start | bytes 131072 | tf_op jit(solution)/shard_map/all_to_all | solution.py:32
  30.1 17.4 %all-to-all-start.1 = ((f16[8,64,256]{2,1,0:T(8,128)(2,1)}), f16[8,64,256]{2,1,0:T(8,128)(2,1)S(1)}, u32[]{:S(2)}, u32[]{:S(2)}) async-start(f16[8,64,256]{2,1,0:T(8,128)(2,1)} %broadcast_in_dim.23), calls=%async_computation.1 | async-start | bytes 524288 | tf_op jit(solution)/shard_map/all_to_all | solution.py:32
  38.4 40.2 %copy-start = (f32[4,256]{1,0:T(4,128)S(1)}, f32[4,256]{1,0:T(4,128)}, u32[]{:S(2)}) copy-start(f32[4,256]{1,0:T(4,128)} %param.9) | copy-start | bytes 12292
  38.4 10.1 %collective-permute-start.2 = (bf16[64,256]{1,0:T(8,128)(2,1)S(1)}, bf16[64,256]{1,0:T(8,128)(2,1)S(1)}, u32[]{:S(2)}, u32[]{:S(2)}) collective-permute-start(bf16[64,256]{1,0:T(8,128)(2,1)S(1)} %convert_element_type.51.rest_1_), channel_id=1, source_target_pairs={{0,48},{16,0},{32,16},{48,32},{1,49},{17,1},{33,17},{49,33},{2,50}... | collective-permute-start | bytes 98312 | tf_op jit(solution)/shard_map/ppermute | solution.py:198
  40.5 7.9 %collective-permute-start.1 = (bf16[64,256]{1,0:T(8,128)(2,1)S(1)}, bf16[64,256]{1,0:T(8,128)(2,1)S(1)}, u32[]{:S(2)}, u32[]{:S(2)}) collective-permute-start(bf16[64,256]{1,0:T(8,128)(2,1)S(1)} %convert_element_type.51.rest_1_), channel_id=1, source_target_pairs={{0,32},{16,48},{32,0},{48,16},{1,33},{17,49},{33,1},{49,17},{2,34}... | collective-permute-start | bytes 98312 | tf_op jit(solution)/shard_map/ppermute | solution.py:198
  43.2 6.9 %collective-permute-start = (bf16[64,256]{1,0:T(8,128)(2,1)S(1)}, bf16[64,256]{1,0:T(8,128)(2,1)S(1)}, u32[]{:S(2)}, u32[]{:S(2)}) collective-permute-start(bf16[64,256]{1,0:T(8,128)(2,1)S(1)} %convert_element_type.51.rest_1_), channel_id=1, source_target_pairs={{0,16},{16,32},{32,48},{48,0},{1,17},{17,33},{33,49},{49,1},{2,18}... | collective-permute-start | bytes 98312 | tf_op jit(solution)/shard_map/ppermute | solution.py:198

commit v5 on v3

--- a/solution.py
+++ b/solution.py
@@ -78,10 +78,6 @@
     )(live, pltpu.with_memory_space_constraint(counts, pltpu.HBM))
 
 
-def block_order(eighth, half):
-    return half * 8 + eighth
-
-
 def prep_kernel(coords, live, both, rows_c, mass):
     rows_c[...] = jnp.swapaxes(both[:, 32:, :].reshape(R, R), 0, 1)
     mass[...] = jnp.zeros_like(mass)
@@ -113,37 +109,49 @@
     )(coords, live, both)
 
 
-def pass_kernel(coords, live, hits, factor, both, rows_c, out, panel):
+def pass_kernel(coords, live, hits, factor, both, rows_c, out, *panels):
     out[...] = jnp.zeros_like(out)
 
-    def step(slot, carry):
-        i = coords[slot * 3]
+    def build(slot, panel):
         j = coords[slot * 3 + 1]
-        k = coords[slot * 3 + 2]
-        piece_a = factor[aligned(i, BS), :]
-        piece_c = rows_c[aligned(k, BS), :]
+        piece_c = rows_c[aligned(coords[slot * 3 + 2], BS), :]
         for half in range(2):
-            for eighth in range(8):
-                rows_b = both[eighth, aligned(j, 8), :]
-                first = block_order(eighth, half) * 4
+            for sender in range(8):
+                rows_b = both[sender, aligned(j, 8), :]
                 for q in range(4):
+                    at = ((half * 8 + sender) * 4 + q) * BS
                     row = rows_b[half * 4 + q : half * 4 + q + 1, :]
-                    panel[(first + q) * BS : (first + q + 1) * BS, :] = (
-                        row * piece_c
-                    ).astype(BF16)
-        total = jnp.zeros((BS, R), F32)
+                    panel[at : at + BS, :] = (row * piece_c).astype(BF16)
+
+    def together(first, many):
+        rows = [factor[aligned(coords[(first + u) * 3], BS), :] for u in range(many)]
+        total = [jnp.zeros((BS, R), F32)] * many
+        for u in range(many):
+            build(first + u, panels[u])
         for start in range(0, BS * BS, SPAN):
-            piece = panel[start : start + SPAN, :]
-            model = lax.dot_general(
-                piece_a, piece, (((1,), (1,)), ((), ())), preferred_element_type=F32
-            )
-            count = hits[slot, :, start : start + SPAN].astype(F32)
-            ratio = (count / model).astype(BF16)
-            total = total + jnp.dot(ratio, piece, preferred_element_type=F32)
-        out[i] = out[i] + total * (piece_a.astype(F32) * PHI_SCALE)
-        return carry
-
-    lax.fori_loop(0, live[0], step, 0)
+            for u in range(many):
+                piece = panels[u][start : start + SPAN, :]
+                model = lax.dot_general(
+                    rows[u], piece, (((1,), (1,)), ((), ())), preferred_element_type=F32
+                )
+                count = hits[first + u, :, start : start + SPAN].astype(F32)
+                ratio = (count / model).astype(BF16)
+                total[u] = total[u] + jnp.dot(ratio, piece, preferred_element_type=F32)
+        for u in range(many):
+            i = coords[(first + u) * 3]
+            out[i] = out[i] + total[u] * (rows[u].astype(F32) * PHI_SCALE)
+
+    @pl.when(live[0] == SLOTS)
+    def _():
+        together(0, SLOTS)
+
+    @pl.when(live[0] < SLOTS)
+    def _():
+        def step(slot, carry):
+            together(slot, 1)
+            return carry
+
+        lax.fori_loop(0, live[0], step, 0)
 
 
 def run_pass(coords, live, hits, factor, both, rows_c):
@@ -151,9 +159,9 @@
         pass_kernel,
         in_specs=[scalars(), scalars()] + [whole()] * 4,
         out_specs=whole(),
-        scratch_shapes=[pltpu.VMEM((BS * BS, R), BF16)],
+        scratch_shapes=[pltpu.VMEM((BS * BS, R), BF16)] * SLOTS,
         out_shape=jax.ShapeDtypeStruct((RB1, BS, R), F32),
-        compiler_params=pltpu.CompilerParams(vmem_limit_bytes=16 << 20),
+        compiler_params=pltpu.CompilerParams(vmem_limit_bytes=24 << 20),
         name="one_pass",
     )(coords, live, hits, factor, both, rows_c)
 
@@ -177,7 +185,8 @@
     both = from_everyone(
         jnp.concatenate([share_b.reshape(32, R), factor_c.T.astype(F16)], axis=0), IA
     ).astype(F32)
-    low = from_everyone(column[:, :4].reshape(64, R).astype(BF16), JX).reshape(R, R)
+    own = column[:, :4].reshape(BS, R).astype(BF16)
+    low = lax.all_gather(own, JX, axis=0, tiled=True)
     rows_c, mass = prepare(coords, live, both)
 
     phi = run_pass(coords, live, hits, low, both, rows_c)

time: 126 us -> 125 us (level)
  blocking collectives: 61.8 us -> 73.6 us
  waiting for transfers between devices: 18.7 us -> 12 us
  starting transfers between devices: 24.4 us -> 19.7 us
  Pallas kernels: 13.5 us -> 12.2 us
    all_gather x0 -> x1, blocking collectives: none -> 12 us  [local(): low = lax.all_gather(own, JX, axis=0, tiled=True)]
    all_to_all x3 -> x2, waiting for transfers between devices: 18.7 us -> 12 us  [swap(): return lax.all_to_all(x, axis, split_axis=0, concat_axis=0, tiled=True)]
    all_to_all x3 -> x2, starting transfers between devices: 24.4 us -> 19.7 us  [swap(): return lax.all_to_all(x, axis, split_axis=0, concat_axis=0, tiled=True)]
    pallas_call x2, Pallas kernels: 10.5 us -> 9.15 us  [run_pass(): pl.pallas_call(pass_kernel, in_specs=[scalars(), scalars()] + [whole()] *...]
  transfers between devices with their start and end apart: 3 -> 2, of which waited for: 3 -> 1; matrix products, arithmetic and copies ran while one was open for 1% -> 1% of each run, Pallas kernels for 2% -> 2%
where the time goes in v5:
time: 125 us; the launch traced here: 123 us
  blocking collectives  73.6 us (59%)
  starting transfers between devices  19.7 us (16%)
  Pallas kernels  12.2 us (10%)
  waiting for transfers between devices  12 us (10%)
  other arithmetic  2.73 us (2%)
  local copies, waits for them, and re-layouts  2.52 us (2%)
    all_to_all x3, blocking collectives, swap(): return lax.all_to_all(x, axis, split_axis=0, concat_axis=0, tiled=True)  61.5 us
    all_to_all x2, starting transfers between devices, swap(): return lax.all_to_all(x, axis, split_axis=0, concat_axis=0, tiled=True)  19.7 us
    all_gather x1, blocking collectives, local(): low = lax.all_gather(own, JX, axis=0, tiled=True)  12 us
    all_to_all x2, waiting for transfers between devices, swap(): return lax.all_to_all(x, axis, split_axis=0, concat_axis=0, tiled=True)  12 us
    pallas_call x2, Pallas kernels, run_pass(): pl.pallas_call(pass_kernel, in_specs=[scalars(), scalars()] + [whole()] *...  9.15 us
  transfers between devices with their start and end apart: 2, of which 1 were waited for; matrix products, arithmetic and copies ran while one was open for 1% of the time, Pallas kernels for 2%

profile of v5, /device:TPU:6, one launch (start us, length us, event | category | flops | bytes accessed | tf_op | source)
XLA Modules:
  0.0 123.5 jit_solution(8075380669000900812)
XLA Ops:
  0.0 0.7 reduce-precision_convert_fusion
  0.7 0.6 broadcast_in_dim.22
  1.4 15.2 %all-to-all-start = ((f16[16,8,256]{2,1,0:T(8,128)(2,1)}), f16[16,8,256]{2,1,0:T(8,128)(2,1)S(1)}, u32[]{:S(2)}, u32[]{:S(2)}) async-start(f16[16,8,256]{2,1,0:T(8,128)(2,1)} %broadcast_in_dim.22), calls=%async_computation | async-start | bytes 131072 | tf_op jit(solution)/shard_map/all_to_all | solution.py:29
  16.6 0.8 convert_bitcast_fusion
  17.3 12.0 %all-to-all-done = f16[16,8,256]{2,1,0:T(8,128)(2,1)S(1)} async-done(((f16[16,8,256]{2,1,0:T(8,128)(2,1)}), f16[16,8,256]{2,1,0:T(8,128)(2,1)S(1)}, u32[]{:S(2)}, u32[]{:S(2)}) %all-to-all-start) | async-done | bytes 65568 | tf_op jit(solution)/shard_map/all_to_all | solution.py:29
  29.4 0.7 broadcast_in_dim.23
  30.1 4.5 %all-to-all-start.1 = ((f16[8,64,256]{2,1,0:T(8,128)(2,1)}), f16[8,64,256]{2,1,0:T(8,128)(2,1)S(1)}, u32[]{:S(2)}, u32[]{:S(2)}) async-start(f16[8,64,256]{2,1,0:T(8,128)(2,1)} %broadcast_in_dim.23), calls=%async_computation.1 | async-start | bytes 524288 | tf_op jit(solution)/shard_map/all_to_all | solution.py:29
  35.2 0.8 copy.11
  36.0 0.1 reshape.49.coords
  36.1 2.3 %load.1.hits = bf16[4,64,4096]{2,1,0:T(8,128)(2,1)S(1)} custom-call(s32[1]{0:T(128)} %bitcast.10.live, s32[4,64,4096]{2,1,0:T(8,128)} %bitcast.14), custom_call_target="tpu_custom_call" | custom-call | tf_op jit(solution)/shard_map/load/pallas_call | solution.py:67
  38.3 0.0 copy-start
  38.4 12.0 %all_gather.3.factor = bf16[256,256]{1,0:T(8,128)(2,1)S(1)} all-gather(bf16[64,256]{1,0:T(8,128)(2,1)S(1)} %convert_element_type.49), channel_id=1, replica_groups=mesh['ia'=8,'jx'=4,'jz'=2,'ka'=8] {'jx'}, dimensions={0}, use_global_device_ids=true | all-gather | bytes 163840 | tf_op jit(solution)/shard_map/all_gather | solution.py:189
  50.4 0.0 all-to-all-done.1
  50.5 0.8 prepare.1
  51.3 4.6 %one_pass.2 = f32[4,64,256]{2,1,0:T(8,128)S(1)} custom-call(s32[12]{0:T(128)S(1)} %reshape.49.coords, s32[1]{0:T(128)} %bitcast.12.live, bf16[4,64,4096]{2,1,0:T(8,128)(2,1)S(1)} %load.1.hits, bf16[256,256]{1,0:T(8,128)(2,1)S(1)} %all_gather.3.factor, f32[8,64,256]{2,1,0:T(8,128)S(1)} %convert_element_type.52.both, f32[256,256]{1,0:T(8,128)S(1)} %get-tuple-element.7.rows_c), custom_call_target="tpu_custom_call" | custom-call | tf_op jit(solution)/shard_map/one_pass/pallas_call | solution.py:158
  55.9 0.1 reshape.53
  56.0 0.2 pad_maximum_fusion
  56.3 20.8 %all_to_all.25 = f16[64,2,640]{2,1,0:T(2,128)(2,1)S(1)} all-to-all(f16[64,2,640]{2,1,0:T(2,128)(2,1)S(1)} %pad_maximum_fusion), channel_id=1, replica_groups=mesh['ia'=8,'jx'=4,'jz'=2,'ka'=8] {'jx','jz','ka'}, dimensions={0} | all-to-all | bytes 327680 | tf_op jit(solution)/shard_map/all_to_all | solution.py:29
  77.0 0.2 convert_reduce_fusion
  77.2 0.0 copy-done
  77.3 20.6 %all_to_all.26 = bf16[64,4,256]{2,1,0:T(4,128)(2,1)S(1)} all-to-all(bf16[64,4,256]{2,1,0:T(4,128)(2,1)S(1)} %broadcast_in_dim.25), channel_id=1, replica_groups=mesh['ia'=8,'jx'=4,'jz'=2,'ka'=8] {'jx','jz','ka'}, dimensions={0} | all-to-all | bytes 262144 | tf_op jit(solution)/shard_map/all_to_all | solution.py:29
  97.9 4.6 %one_pass.3 = f32[4,64,256]{2,1,0:T(8,128)S(1)} custom-call(s32[12]{0:T(128)S(1)} %reshape.49.coords, s32[1]{0:T(128)} %bitcast.13.live, bf16[4,64,4096]{2,1,0:T(8,128)(2,1)S(1)} %load.1.hits, bf16[256,256]{1,0:T(8,128)(2,1)S(1)} %reshape.56.factor, f32[8,64,256]{2,1,0:T(8,128)S(1)} %convert_element_type.52.both, f32[256,256]{1,0:T(8,128)S(1)} %get-tuple-element.7.rows_c), custom_call_target="tpu_custom_call" | custom-call | tf_op jit(solution)/shard_map/one_pass/pallas_call | solution.py:158
  102.5 20.2 %all_to_all.27 = f16[64,4,256]{2,1,0:T(4,128)(2,1)S(1)} all-to-all(f16[64,4,256]{2,1,0:T(4,128)(2,1)S(1)} %reshape.57), channel_id=1, replica_groups=mesh['ia'=8,'jx'=4,'jz'=2,'ka'=8] {'jx','jz','ka'}, dimensions={0} | all-to-all | bytes 262144 | tf_op jit(solution)/shard_map/all_to_all | solution.py:29
  122.8 0.1 convert_reduce_fusion.1
  122.9 0.6 fusion.4
  (20 shorter events, 0.4 us)
Async XLA Ops:
  1.4 27.9 %all-to-all-start = ((f16[16,8,256]{2,1,0:T(8,128)(2,1)}), f16[16,8,256]{2,1,0:T(8,128)(2,1)S(1)}, u32[]{:S(2)}, u32[]{:S(2)}) async-start(f16[16,8,256]{2,1,0:T(8,128)(2,1)} %broadcast_in_dim.22), calls=%async_computation | async-start | bytes 131072 | tf_op jit(solution)/shard_map/all_to_all | solution.py:29
  30.1 20.3 %all-to-all-start.1 = ((f16[8,64,256]{2,1,0:T(8,128)(2,1)}), f16[8,64,256]{2,1,0:T(8,128)(2,1)S(1)}, u32[]{:S(2)}, u32[]{:S(2)}) async-start(f16[8,64,256]{2,1,0:T(8,128)(2,1)} %broadcast_in_dim.23), calls=%async_computation.1 | async-start | bytes 524288 | tf_op jit(solution)/shard_map/all_to_all | solution.py:29
  38.3 38.9 %copy-start = (f32[4,256]{1,0:T(4,128)S(1)}, f32[4,256]{1,0:T(4,128)}, u32[]{:S(2)}) copy-start(f32[4,256]{1,0:T(4,128)} %param.9) | copy-start | bytes 12292

commit v6 on v5

--- a/solution.py
+++ b/solution.py
@@ -1,3 +1,5 @@
+import functools
+
 import jax
 import jax.numpy as jnp
 from jax import lax
@@ -21,7 +23,8 @@
 JX = "jx"
 JZ = "jz"
 KA = "ka"
-JK = (JX, JZ, KA)
+ALL = (JZ, JX, KA)
+HALF = BS // 2
 ZK = (JZ, KA)
 
 
@@ -109,7 +112,7 @@
     )(coords, live, both)
 
 
-def pass_kernel(coords, live, hits, factor, both, rows_c, out, *panels):
+def pass_kernel(halves, coords, live, hits, factor, both, rows_c, out, *panels):
     out[...] = jnp.zeros_like(out)
 
     def build(slot, panel):
@@ -123,8 +126,15 @@
                     row = rows_b[half * 4 + q : half * 4 + q + 1, :]
                     panel[at : at + BS, :] = (row * piece_c).astype(BF16)
 
+    def factor_rows(i):
+        if not halves:
+            return factor[aligned(i, BS), :]
+        return jnp.concatenate(
+            [factor[aligned(i + RB1 * jz, HALF), :] for jz in range(2)], axis=0
+        )
+
     def together(first, many):
-        rows = [factor[aligned(coords[(first + u) * 3], BS), :] for u in range(many)]
+        rows = [factor_rows(coords[(first + u) * 3]) for u in range(many)]
         total = [jnp.zeros((BS, R), F32)] * many
         for u in range(many):
             build(first + u, panels[u])
@@ -139,7 +149,9 @@
                 total[u] = total[u] + jnp.dot(ratio, piece, preferred_element_type=F32)
         for u in range(many):
             i = coords[(first + u) * 3]
-            out[i] = out[i] + total[u] * (rows[u].astype(F32) * PHI_SCALE)
+            part = total[u] * (rows[u].astype(F32) * PHI_SCALE)
+            out[0, i] = out[0, i] + part[:HALF]
+            out[1, i] = out[1, i] + part[HALF:]
 
     @pl.when(live[0] == SLOTS)
     def _():
@@ -154,13 +166,13 @@
         lax.fori_loop(0, live[0], step, 0)
 
 
-def run_pass(coords, live, hits, factor, both, rows_c):
+def run_pass(halves, coords, live, hits, factor, both, rows_c):
     return pl.pallas_call(
-        pass_kernel,
+        functools.partial(pass_kernel, halves),
         in_specs=[scalars(), scalars()] + [whole()] * 4,
         out_specs=whole(),
         scratch_shapes=[pltpu.VMEM((BS * BS, R), BF16)] * SLOTS,
-        out_shape=jax.ShapeDtypeStruct((RB1, BS, R), F32),
+        out_shape=jax.ShapeDtypeStruct((2, RB1, HALF, R), F32),
         compiler_params=pltpu.CompilerParams(vmem_limit_bytes=24 << 20),
         name="one_pass",
     )(coords, live, hits, factor, both, rows_c)
@@ -179,7 +191,9 @@
     live = live_blocks.reshape(1)
     low_a = rounded(factor_a)
     mine_b = lax.dynamic_slice_in_dim(factor_b, lax.axis_index(IA) * 4, 4, 0)
-    column = from_everyone(jnp.concatenate([low_a.astype(F16), mine_b.astype(F16)], axis=0), ZK)
+    column = from_everyone(
+        jnp.concatenate([low_a.astype(F16), mine_b.astype(F16)], axis=0), ZK
+    )
     hits = load(live, counts.reshape(SLOTS, BS, BS * BS))
     share_b = lax.dynamic_slice_in_dim(column[:, 4:], lax.axis_index(JZ) * 8, 8, 0)
     both = from_everyone(
@@ -189,18 +203,19 @@
     low = lax.all_gather(own, JX, axis=0, tiled=True)
     rows_c, mass = prepare(coords, live, both)
 
-    phi = run_pass(coords, live, hits, low, both, rows_c)
+    phi = run_pass(False, coords, live, hits, low, both, rows_c)
     mass_rows = jnp.broadcast_to(
-        (mass[:, 0, :] * MASS_SCALE).astype(F16).reshape(RB1, 1, 2, 128), (RB1, 16, 2, 128)
+        (mass[:, 0, :] * MASS_SCALE).astype(F16).reshape(1, RB1, 1, 2, 128),
+        (2, RB1, 8, 2, 128),
     ).reshape(64, 2, 128)
     sent = jnp.concatenate([phi.astype(F16).reshape(64, 2, 512), mass_rows], axis=2)
-    got = swap(sent, JK).astype(F32).sum(axis=0)
+    got = swap(sent, ALL).astype(F32).sum(axis=0)
     scale = (MASS_SCALE / PHI_SCALE) / got[:, 512:].reshape(1, R)
     first = unweighted(factor_a, low_a) * got[:, :512].reshape(4, R) * scale
     low_first = rounded(first)
-    low = from_everyone(low_first.astype(BF16), JK).reshape(R, R)
-    phi = run_pass(coords, live, hits, low, both, rows_c)
-    mine = swap(phi.astype(F16).reshape(64, 4, R), JK).astype(F32).sum(axis=0)
+    low = from_everyone(low_first.astype(BF16), ALL).reshape(R, R)
+    phi = run_pass(True, coords, live, hits, low, both, rows_c)
+    mine = swap(phi.astype(F16).reshape(64, 4, R), ALL).astype(F32).sum(axis=0)
     return unweighted(first, low_first) * mine * scale
 
 

time: 125 us -> 126 us (level)
  the two profiles are of different devices: /device:TPU:6 before, /device:TPU:8 now
where the time goes in v6:
time: 126 us
  blocking collectives  79.1 us (63%)
  starting transfers between devices  20.1 us (16%)
  waiting for transfers between devices  12 us (10%)
  Pallas kernels  8.21 us (7%)
  other arithmetic  2.73 us (2%)
  local copies, waits for them, and re-layouts  2.52 us (2%)
    all_to_all x3, blocking collectives, swap(): return lax.all_to_all(x, axis, split_axis=0, concat_axis=0, tiled=True)  66.8 us
    all_to_all x2, starting transfers between devices, swap(): return lax.all_to_all(x, axis, split_axis=0, concat_axis=0, tiled=True)  20.1 us
    all_gather x1, blocking collectives, local(): low = lax.all_gather(own, JX, axis=0, tiled=True)  12.3 us
    all_to_all x2, waiting for transfers between devices, swap(): return lax.all_to_all(x, axis, split_axis=0, concat_axis=0, tiled=True)  12 us
    pallas_call x2, Pallas kernels, run_pass(): pl.pallas_call(functools.partial(pass_kernel, halves), in_specs=[scalars(...  5.83 us
  transfers between devices with their start and end apart: 2, of which 1 were waited for; matrix products, arithmetic and copies ran while one was open for 1% of the time, Pallas kernels for 1%

profile of v6, /device:TPU:8, one launch (start us, length us, event | category | flops | bytes accessed | tf_op | source)
XLA Modules:
  0.0 125.5 jit_solution(12814934922186191933)
XLA Ops:
  0.0 0.7 reduce-precision_convert_fusion
  0.7 0.6 broadcast_in_dim.22
  1.4 15.2 %all-to-all-start = ((f16[16,8,256]{2,1,0:T(8,128)(2,1)}), f16[16,8,256]{2,1,0:T(8,128)(2,1)S(1)}, u32[]{:S(2)}, u32[]{:S(2)}) async-start(f16[16,8,256]{2,1,0:T(8,128)(2,1)} %broadcast_in_dim.22), calls=%async_computation | async-start | bytes 131072 | tf_op jit(solution)/shard_map/all_to_all | solution.py:32
  16.6 0.8 convert_bitcast_fusion
  17.3 12.0 %all-to-all-done = f16[16,8,256]{2,1,0:T(8,128)(2,1)S(1)} async-done(((f16[16,8,256]{2,1,0:T(8,128)(2,1)}), f16[16,8,256]{2,1,0:T(8,128)(2,1)S(1)}, u32[]{:S(2)}, u32[]{:S(2)}) %all-to-all-start) | async-done | bytes 65568 | tf_op jit(solution)/shard_map/all_to_all | solution.py:32
  29.4 0.7 broadcast_in_dim.23
  30.1 4.9 %all-to-all-start.1 = ((f16[8,64,256]{2,1,0:T(8,128)(2,1)}), f16[8,64,256]{2,1,0:T(8,128)(2,1)S(1)}, u32[]{:S(2)}, u32[]{:S(2)}) async-start(f16[8,64,256]{2,1,0:T(8,128)(2,1)} %broadcast_in_dim.23), calls=%async_computation.1 | async-start | bytes 524288 | tf_op jit(solution)/shard_map/all_to_all | solution.py:32
  35.7 0.8 copy.11
  36.4 0.1 reshape.49.coords
  36.5 1.6 %load.1.hits = bf16[4,64,4096]{2,1,0:T(8,128)(2,1)S(1)} custom-call(s32[1]{0:T(128)} %bitcast.14.live, s32[4,64,4096]{2,1,0:T(8,128)} %bitcast.18), custom_call_target="tpu_custom_call" | custom-call | tf_op jit(solution)/shard_map/load/pallas_call | solution.py:70
  38.2 0.0 copy-start
  38.2 12.3 %all_gather.3.factor = bf16[256,256]{1,0:T(8,128)(2,1)S(1)} all-gather(bf16[64,256]{1,0:T(8,128)(2,1)S(1)} %convert_element_type.49), channel_id=1, replica_groups=mesh['ia'=8,'jx'=4,'jz'=2,'ka'=8] {'jx'}, dimensions={0}, use_global_device_ids=true | all-gather | bytes 163840 | tf_op jit(solution)/shard_map/all_gather | solution.py:203
  50.5 0.0 all-to-all-done.1
  50.6 0.7 prepare.1
  51.4 2.9 %one_pass.2 = f32[2,4,32,256]{3,2,1,0:T(8,128)S(1)} custom-call(s32[12]{0:T(128)S(1)} %reshape.49.coords, s32[1]{0:T(128)} %bitcast.16.live, bf16[4,64,4096]{2,1,0:T(8,128)(2,1)S(1)} %load.1.hits, bf16[256,256]{1,0:T(8,128)(2,1)S(1)} %all_gather.3.factor, f32[8,64,256]{2,1,0:T(8,128)S(1)} %convert_element_type.52.both, f32[256,256]{1,0:T(8,128)S(1)} %get-tuple-element.7.rows_c), custom_call_target="tpu_custom_call" | custom-call | tf_op jit(solution)/shard_map/one_pass/pallas_call | solution.py:170
  54.3 0.1 reshape.53
  54.5 0.2 pad_maximum_fusion
  54.7 24.6 %all_to_all.25 = f16[64,2,640]{2,1,0:T(2,128)(2,1)S(1)} all-to-all(f16[64,2,640]{2,1,0:T(2,128)(2,1)S(1)} %pad_maximum_fusion), channel_id=1, replica_groups=mesh['ia'=8,'jx'=4,'jz'=2,'ka'=8] {'jz','jx','ka'}, dimensions={0} | all-to-all | bytes 327680 | tf_op jit(solution)/shard_map/all_to_all | solution.py:32
  79.3 0.2 convert_reduce_fusion
  79.5 0.0 copy-done
  79.6 20.4 %all_to_all.26 = bf16[64,4,256]{2,1,0:T(4,128)(2,1)S(1)} all-to-all(bf16[64,4,256]{2,1,0:T(4,128)(2,1)S(1)} %broadcast_in_dim.25), channel_id=1, replica_groups=mesh['ia'=8,'jx'=4,'jz'=2,'ka'=8] {'jz','jx','ka'}, dimensions={0} | all-to-all | bytes 262144 | tf_op jit(solution)/shard_map/all_to_all | solution.py:32
  100.0 2.9 %one_pass.3 = f32[2,4,32,256]{3,2,1,0:T(8,128)S(1)} custom-call(s32[12]{0:T(128)S(1)} %reshape.49.coords, s32[1]{0:T(128)} %bitcast.17.live, bf16[4,64,4096]{2,1,0:T(8,128)(2,1)S(1)} %load.1.hits, bf16[256,256]{1,0:T(8,128)(2,1)S(1)} %reshape.56.factor, f32[8,64,256]{2,1,0:T(8,128)S(1)} %convert_element_type.52.both, f32[256,256]{1,0:T(8,128)S(1)} %get-tuple-element.7.rows_c), custom_call_target="tpu_custom_call" | custom-call | tf_op jit(solution)/shard_map/one_pass/pallas_call | solution.py:170
  103.0 21.8 %all_to_all.27 = f16[64,4,256]{2,1,0:T(4,128)(2,1)S(1)} all-to-all(f16[64,4,256]{2,1,0:T(4,128)(2,1)S(1)} %reshape.57), channel_id=1, replica_groups=mesh['ia'=8,'jx'=4,'jz'=2,'ka'=8] {'jz','jx','ka'}, dimensions={0} | all-to-all | bytes 262144 | tf_op jit(solution)/shard_map/all_to_all | solution.py:32
  124.8 0.1 convert_reduce_fusion.1
  124.9 0.6 fusion.4
  (20 shorter events, 0.4 us)
Async XLA Ops:
  1.4 27.9 %all-to-all-start = ((f16[16,8,256]{2,1,0:T(8,128)(2,1)}), f16[16,8,256]{2,1,0:T(8,128)(2,1)S(1)}, u32[]{:S(2)}, u32[]{:S(2)}) async-start(f16[16,8,256]{2,1,0:T(8,128)(2,1)} %broadcast_in_dim.22), calls=%async_computation | async-start | bytes 131072 | tf_op jit(solution)/shard_map/all_to_all | solution.py:32
  30.1 20.4 %all-to-all-start.1 = ((f16[8,64,256]{2,1,0:T(8,128)(2,1)}), f16[8,64,256]{2,1,0:T(8,128)(2,1)S(1)}, u32[]{:S(2)}, u32[]{:S(2)}) async-start(f16[8,64,256]{2,1,0:T(8,128)(2,1)} %broadcast_in_dim.23), calls=%async_computation.1 | async-start | bytes 524288 | tf_op jit(solution)/shard_map/all_to_all | solution.py:32
  38.2 41.4 %copy-start = (f32[4,256]{1,0:T(4,128)S(1)}, f32[4,256]{1,0:T(4,128)}, u32[]{:S(2)}) copy-start(f32[4,256]{1,0:T(4,128)} %param.9) | copy-start | bytes 12292

commit v7 on v5

--- a/solution.py
+++ b/solution.py
@@ -1,3 +1,5 @@
+import functools
+
 import jax
 import jax.numpy as jnp
 from jax import lax
@@ -16,6 +18,7 @@
 PHI_SCALE = 0.25
 MASS_SCALE = 1.0 / 32.0
 BF16 = jnp.bfloat16
+
 
 IA = "ia"
 JX = "jx"
@@ -109,7 +112,14 @@
     )(coords, live, both)
 
 
-def pass_kernel(coords, live, hits, factor, both, rows_c, out, *panels):
+def pass_kernel(split, coords, live, hits, both, rows_c, *rest):
+    if split:
+        place, *parts, out, factor = rest[: RB1 + 3]
+        panels = rest[RB1 + 3 :]
+        for back in range(RB1):
+            factor[back * BS : (back + 1) * BS, :] = parts[back][...]
+    else:
+        factor, out, *panels = rest
     out[...] = jnp.zeros_like(out)
 
     def build(slot, panel):
@@ -123,8 +133,12 @@
                     row = rows_b[half * 4 + q : half * 4 + q + 1, :]
                     panel[at : at + BS, :] = (row * piece_c).astype(BF16)
 
+    def factor_rows(i):
+        at = (place[0] - i) & (RB1 - 1) if split else i
+        return factor[aligned(at, BS), :]
+
     def together(first, many):
-        rows = [factor[aligned(coords[(first + u) * 3], BS), :] for u in range(many)]
+        rows = [factor_rows(coords[(first + u) * 3]) for u in range(many)]
         total = [jnp.zeros((BS, R), F32)] * many
         for u in range(many):
             build(first + u, panels[u])
@@ -154,16 +168,21 @@
         lax.fori_loop(0, live[0], step, 0)
 
 
-def run_pass(coords, live, hits, factor, both, rows_c):
+def run_pass(coords, live, hits, both, rows_c, place, *factor):
+    split = place is not None
+    extra = [place] if split else []
+    scratch = [pltpu.VMEM((R, R), BF16)] if split else []
     return pl.pallas_call(
-        pass_kernel,
-        in_specs=[scalars(), scalars()] + [whole()] * 4,
+        functools.partial(pass_kernel, split),
+        in_specs=[scalars(), scalars(), whole(), whole(), whole()]
+        + [scalars()] * len(extra)
+        + [whole()] * len(factor),
         out_specs=whole(),
-        scratch_shapes=[pltpu.VMEM((BS * BS, R), BF16)] * SLOTS,
+        scratch_shapes=scratch + [pltpu.VMEM((BS * BS, R), BF16)] * SLOTS,
         out_shape=jax.ShapeDtypeStruct((RB1, BS, R), F32),
         compiler_params=pltpu.CompilerParams(vmem_limit_bytes=24 << 20),
         name="one_pass",
-    )(coords, live, hits, factor, both, rows_c)
+    )(coords, live, hits, both, rows_c, *extra, *factor)
 
 
 def rounded(x):
@@ -186,10 +205,13 @@
         jnp.concatenate([share_b.reshape(32, R), factor_c.T.astype(F16)], axis=0), IA
     ).astype(F32)
     own = column[:, :4].reshape(BS, R).astype(BF16)
-    low = lax.all_gather(own, JX, axis=0, tiled=True)
+    pieces = {0: own}
+    for back in (2, 1, 3):
+        pieces[back] = lax.ppermute(own, JX, [(x, (x + back) % 4) for x in range(4)])
     rows_c, mass = prepare(coords, live, both)
 
-    phi = run_pass(coords, live, hits, low, both, rows_c)
+    place = lax.axis_index(JX).reshape(1)
+    phi = run_pass(coords, live, hits, both, rows_c, place, *[pieces[d] for d in range(4)])
     mass_rows = jnp.broadcast_to(
         (mass[:, 0, :] * MASS_SCALE).astype(F16).reshape(RB1, 1, 2, 128), (RB1, 16, 2, 128)
     ).reshape(64, 2, 128)
@@ -199,7 +221,7 @@
     first = unweighted(factor_a, low_a) * got[:, :512].reshape(4, R) * scale
     low_first = rounded(first)
     low = from_everyone(low_first.astype(BF16), JK).reshape(R, R)
-    phi = run_pass(coords, live, hits, low, both, rows_c)
+    phi = run_pass(coords, live, hits, both, rows_c, None, low)
     mine = swap(phi.astype(F16).reshape(64, 4, R), JK).astype(F32).sum(axis=0)
     return unweighted(first, low_first) * mine * scale
 

time: 125 us -> 126 us (level)
  blocking collectives: 73.6 us -> 63.3 us
  starting transfers between devices: 19.7 us -> 28.8 us
  waiting for transfers between devices: 12 us -> 13.6 us
    all_gather x1 -> x0, blocking collectives: 12 us -> none  [local(): low = lax.all_gather(own, JX, axis=0, tiled=True)]
    ppermute x0 -> x3, starting transfers between devices: none -> 9.13 us  [local(): lax.ppermute(own, JX, [(x, (x + back) % 4) for x in range(4)])]
    all_to_all x3, blocking collectives: 61.5 us -> 63.3 us  [swap(): return lax.all_to_all(x, axis, split_axis=0, concat_axis=0, tiled=True)]
    ppermute x0 -> x3, waiting for transfers between devices: none -> 1.66 us  [local(): lax.ppermute(own, JX, [(x, (x + back) % 4) for x in range(4)])]
  transfers between devices with their start and end apart: 2 -> 5, of which waited for: 1 -> 2; matrix products, arithmetic and copies ran while one was open for 1% -> 1% of each run, Pallas kernels for 2% -> 2%
where the time goes in v7:
time: 126 us; the launch traced here: 124 us
  blocking collectives  63.3 us (50%)
  starting transfers between devices  28.8 us (23%)
  waiting for transfers between devices  13.6 us (11%)
  Pallas kernels  12.2 us (10%)
  other arithmetic  2.73 us (2%)
  local copies, waits for them, and re-layouts  2.55 us (2%)
    all_to_all x3, blocking collectives, swap(): return lax.all_to_all(x, axis, split_axis=0, concat_axis=0, tiled=True)  63.3 us
    all_to_all x2, starting transfers between devices, swap(): return lax.all_to_all(x, axis, split_axis=0, concat_axis=0, tiled=True)  19.7 us
    all_to_all x2, waiting for transfers between devices, swap(): return lax.all_to_all(x, axis, split_axis=0, concat_axis=0, tiled=True)  12 us
    pallas_call x2, Pallas kernels, run_pass(): pl.pallas_call(functools.partial(pass_kernel, split), in_specs=[scalars()...  9.15 us
    ppermute x3, starting transfers between devices, local(): lax.ppermute(own, JX, [(x, (x + back) % 4) for x in range(4)])  9.13 us
  transfers between devices with their start and end apart: 5, of which 2 were waited for; matrix products, arithmetic and copies ran while one was open for 1% of the time, Pallas kernels for 2%

profile of v7, /device:TPU:6, one launch (start us, length us, event | category | flops | bytes accessed | tf_op | source)
XLA Modules:
  0.0 124.1 jit_solution(17135184816204317830)
XLA Ops:
  0.0 0.7 reduce-precision_convert_fusion
  0.7 0.6 broadcast_in_dim.22
  1.4 15.2 %all-to-all-start = ((f16[16,8,256]{2,1,0:T(8,128)(2,1)}), f16[16,8,256]{2,1,0:T(8,128)(2,1)S(1)}, u32[]{:S(2)}, u32[]{:S(2)}) async-start(f16[16,8,256]{2,1,0:T(8,128)(2,1)} %broadcast_in_dim.22), calls=%async_computation | async-start | bytes 131072 | tf_op jit(solution)/shard_map/all_to_all | solution.py:32
  16.6 0.8 convert_bitcast_fusion
  17.3 12.0 %all-to-all-done = f16[16,8,256]{2,1,0:T(8,128)(2,1)S(1)} async-done(((f16[16,8,256]{2,1,0:T(8,128)(2,1)}), f16[16,8,256]{2,1,0:T(8,128)(2,1)S(1)}, u32[]{:S(2)}, u32[]{:S(2)}) %all-to-all-start) | async-done | bytes 65568 | tf_op jit(solution)/shard_map/all_to_all | solution.py:32
  29.4 0.7 broadcast_in_dim.23
  30.1 4.5 %all-to-all-start.1 = ((f16[8,64,256]{2,1,0:T(8,128)(2,1)}), f16[8,64,256]{2,1,0:T(8,128)(2,1)S(1)}, u32[]{:S(2)}, u32[]{:S(2)}) async-start(f16[8,64,256]{2,1,0:T(8,128)(2,1)} %broadcast_in_dim.23), calls=%async_computation.1 | async-start | bytes 524288 | tf_op jit(solution)/shard_map/all_to_all | solution.py:32
  35.2 0.8 copy.11
  36.0 0.1 reshape.52.coords
  36.1 2.3 %load.1.hits = bf16[4,64,4096]{2,1,0:T(8,128)(2,1)S(1)} custom-call(s32[1]{0:T(128)} %bitcast.11.live, s32[4,64,4096]{2,1,0:T(8,128)} %bitcast.15), custom_call_target="tpu_custom_call" | custom-call | tf_op jit(solution)/shard_map/load/pallas_call | solution.py:70
  38.4 0.0 copy-start
  38.4 2.1 %collective-permute-start.2 = (bf16[64,256]{1,0:T(8,128)(2,1)S(1)}, bf16[64,256]{1,0:T(8,128)(2,1)S(1)}, u32[]{:S(2)}, u32[]{:S(2)}) collective-permute-start(bf16[64,256]{1,0:T(8,128)(2,1)S(1)} %convert_element_type.51.rest_1_), channel_id=1, source_target_pairs={{0,48},{16,0},{32,16},{48,32},{1,49},{17,1},{33,17},{49,33},{2,50}... | collective-permute-start | bytes 98312 | tf_op jit(solution)/shard_map/ppermute | solution.py:210
  40.5 2.7 %collective-permute-start.1 = (bf16[64,256]{1,0:T(8,128)(2,1)S(1)}, bf16[64,256]{1,0:T(8,128)(2,1)S(1)}, u32[]{:S(2)}, u32[]{:S(2)}) collective-permute-start(bf16[64,256]{1,0:T(8,128)(2,1)S(1)} %convert_element_type.51.rest_1_), channel_id=1, source_target_pairs={{0,32},{16,48},{32,0},{48,16},{1,33},{17,49},{33,1},{49,17},{2,34}... | collective-permute-start | bytes 98312 | tf_op jit(solution)/shard_map/ppermute | solution.py:210
  43.2 4.3 %collective-permute-start = (bf16[64,256]{1,0:T(8,128)(2,1)S(1)}, bf16[64,256]{1,0:T(8,128)(2,1)S(1)}, u32[]{:S(2)}, u32[]{:S(2)}) collective-permute-start(bf16[64,256]{1,0:T(8,128)(2,1)S(1)} %convert_element_type.51.rest_1_), channel_id=1, source_target_pairs={{0,16},{16,32},{32,48},{48,0},{1,17},{17,33},{33,49},{49,1},{2,18}... | collective-permute-start | bytes 98312 | tf_op jit(solution)/shard_map/ppermute | solution.py:210
  47.6 0.0 all-to-all-done.1
  47.6 0.8 prepare.1
  48.5 0.0 collective-permute-done.2.rest_4_
  48.5 0.0 collective-permute-done.1.rest_3_
  48.5 1.7 %collective-permute-done.rest_2_ = bf16[64,256]{1,0:T(8,128)(2,1)S(1)} collective-permute-done((bf16[64,256]{1,0:T(8,128)(2,1)S(1)}, bf16[64,256]{1,0:T(8,128)(2,1)S(1)}, u32[]{:S(2)}, u32[]{:S(2)}) %collective-permute-start) | collective-permute-done | bytes 32800 | tf_op jit(solution)/shard_map/ppermute | solution.py:210
  50.1 4.6 %one_pass.2 = f32[4,64,256]{2,1,0:T(8,128)S(1)} custom-call(s32[12]{0:T(128)S(1)} %reshape.52.coords, s32[1]{0:T(128)} %bitcast.13.live, bf16[4,64,4096]{2,1,0:T(8,128)(2,1)S(1)} %load.1.hits, f32[8,64,256]{2,1,0:T(8,128)S(1)} %convert_element_type.49.both, f32[256,256]{1,0:T(8,128)S(1)} %get-tuple-element.7.rows_c, s32[1]{0:T(128)} %bitcast.3.rest_0_, ...), custom_call_target="tpu_custom_call" | custom-call | tf_op jit(solution)/shard_map/one_pass/pallas_call | solution.py:175
  54.7 0.1 reshape.57
  54.9 0.2 pad_maximum_fusion
  55.1 22.6 %all_to_all.25 = f16[64,2,640]{2,1,0:T(2,128)(2,1)S(1)} all-to-all(f16[64,2,640]{2,1,0:T(2,128)(2,1)S(1)} %pad_maximum_fusion), channel_id=1, replica_groups=mesh['ia'=8,'jx'=4,'jz'=2,'ka'=8] {'jx','jz','ka'}, dimensions={0} | all-to-all | bytes 327680 | tf_op jit(solution)/shard_map/all_to_all | solution.py:32
  77.7 0.2 convert_reduce_fusion
  77.9 0.0 copy-done
  78.0 20.6 %all_to_all.26 = bf16[64,4,256]{2,1,0:T(4,128)(2,1)S(1)} all-to-all(bf16[64,4,256]{2,1,0:T(4,128)(2,1)S(1)} %broadcast_in_dim.25), channel_id=1, replica_groups=mesh['ia'=8,'jx'=4,'jz'=2,'ka'=8] {'jx','jz','ka'}, dimensions={0} | all-to-all | bytes 262144 | tf_op jit(solution)/shard_map/all_to_all | solution.py:32
  98.6 4.6 %one_pass.3 = f32[4,64,256]{2,1,0:T(8,128)S(1)} custom-call(s32[12]{0:T(128)S(1)} %reshape.52.coords, s32[1]{0:T(128)} %bitcast.14.live, bf16[4,64,4096]{2,1,0:T(8,128)(2,1)S(1)} %load.1.hits, f32[8,64,256]{2,1,0:T(8,128)S(1)} %convert_element_type.49.both, f32[256,256]{1,0:T(8,128)S(1)} %get-tuple-element.7.rows_c, bf16[256,256]{1,0:T(8,128)(2,1)S(1)} %reshape.60.rest_0_), custom_call_target="tpu_custom_call" | custom-call | tf_op jit(solution)/shard_map/one_pass/pallas_call | solution.py:175
  103.3 20.1 %all_to_all.27 = f16[64,4,256]{2,1,0:T(4,128)(2,1)S(1)} all-to-all(f16[64,4,256]{2,1,0:T(4,128)(2,1)S(1)} %reshape.61), channel_id=1, replica_groups=mesh['ia'=8,'jx'=4,'jz'=2,'ka'=8] {'jx','jz','ka'}, dimensions={0} | all-to-all | bytes 262144 | tf_op jit(solution)/shard_map/all_to_all | solution.py:32
  123.4 0.1 convert_reduce_fusion.1
  123.5 0.6 fusion.4
  (20 shorter events, 0.4 us)
Async XLA Ops:
  1.4 27.9 %all-to-all-start = ((f16[16,8,256]{2,1,0:T(8,128)(2,1)}), f16[16,8,256]{2,1,0:T(8,128)(2,1)S(1)}, u32[]{:S(2)}, u32[]{:S(2)}) async-start(f16[16,8,256]{2,1,0:T(8,128)(2,1)} %broadcast_in_dim.22), calls=%async_computation | async-start | bytes 131072 | tf_op jit(solution)/shard_map/all_to_all | solution.py:32
  30.1 17.4 %all-to-all-start.1 = ((f16[8,64,256]{2,1,0:T(8,128)(2,1)}), f16[8,64,256]{2,1,0:T(8,128)(2,1)S(1)}, u32[]{:S(2)}, u32[]{:S(2)}) async-start(f16[8,64,256]{2,1,0:T(8,128)(2,1)} %broadcast_in_dim.23), calls=%async_computation.1 | async-start | bytes 524288 | tf_op jit(solution)/shard_map/all_to_all | solution.py:32
  38.4 39.5 %copy-start = (f32[4,256]{1,0:T(4,128)S(1)}, f32[4,256]{1,0:T(4,128)}, u32[]{:S(2)}) copy-start(f32[4,256]{1,0:T(4,128)} %param.9) | copy-start | bytes 12292
  38.4 10.1 %collective-permute-start.2 = (bf16[64,256]{1,0:T(8,128)(2,1)S(1)}, bf16[64,256]{1,0:T(8,128)(2,1)S(1)}, u32[]{:S(2)}, u32[]{:S(2)}) collective-permute-start(bf16[64,256]{1,0:T(8,128)(2,1)S(1)} %convert_element_type.51.rest_1_), channel_id=1, source_target_pairs={{0,48},{16,0},{32,16},{48,32},{1,49},{17,1},{33,17},{49,33},{2,50}... | collective-permute-start | bytes 98312 | tf_op jit(solution)/shard_map/ppermute | solution.py:210
  40.5 7.9 %collective-permute-start.1 = (bf16[64,256]{1,0:T(8,128)(2,1)S(1)}, bf16[64,256]{1,0:T(8,128)(2,1)S(1)}, u32[]{:S(2)}, u32[]{:S(2)}) collective-permute-start(bf16[64,256]{1,0:T(8,128)(2,1)S(1)} %convert_element_type.51.rest_1_), channel_id=1, source_target_pairs={{0,32},{16,48},{32,0},{48,16},{1,33},{17,49},{33,1},{49,17},{2,34}... | collective-permute-start | bytes 98312 | tf_op jit(solution)/shard_map/ppermute | solution.py:210
  43.2 6.9 %collective-permute-start = (bf16[64,256]{1,0:T(8,128)(2,1)S(1)}, bf16[64,256]{1,0:T(8,128)(2,1)S(1)}, u32[]{:S(2)}, u32[]{:S(2)}) collective-permute-start(bf16[64,256]{1,0:T(8,128)(2,1)S(1)} %convert_element_type.51.rest_1_), channel_id=1, source_target_pairs={{0,16},{16,32},{32,48},{48,0},{1,17},{17,33},{33,49},{49,1},{2,18}... | collective-permute-start | bytes 98312 | tf_op jit(solution)/shard_map/ppermute | solution.py:210
